TPU v7x, 128 devices: a whole 4x4x4 slice. The times are simulated.
128 devices in a mesh: gx: 4 (over z), gy: 4 (over y), gz: 8 (over x, core).
Axes of the slice: x: 4, y: 4, z: 4, core: 2. Of those that a mesh axis runs over, the one named last changes fastest.
Arguments:
- test_vectors: float32 [8, 64, 64, 8192], P(None, 'gx', 'gy', 'gz'), as said below
- aniso: int32 [3, 2], replicated, may hold values from 2 to 4
Outputs:
- basis: float32 [8, 64, 64, 8192], P(None, 'gx', 'gy', 'gz')
- coarse_basis: float32 [8, 32, 32, 4096], P(None, 'gx', 'gy', 'gz')
Inputs may be any that keep to these rules, and one draw needn't show every extreme that they name: `test_vectors`: positive and negative values; every test vector is linearly independent of the others.
All inputs are finite; a program needn't handle non-finite values.
Results may differ from a plain program's by a relative error of at most 0.00029.
Values sent between devices are 32-bit elements; how exact they have to be, the bound alone decides.
A program may use at most 384 MiB of HBM per device.

v0:
```python
import functools

import jax
import jax.numpy as jnp
from jax import lax
from jax.sharding import Mesh
from jax.sharding import PartitionSpec as P

GX_GY_GZ = ("gx", "gy", "gz_0", "gz_1")
GZ = ("gz_0", "gz_1")


omega_weight = 2.0 / 3.0


def with_halo(shard, sides, width):
    edges = {}
    for axis, dim in sides:
        count, length = (lax.axis_size(axis), shard.shape[dim])
        up = [(i, (i + 1) % count) for i in range(count - 1)]
        last = lax.slice_in_dim(shard, length - width, length, axis=dim)
        initial = lax.slice_in_dim(shard, 0, width, axis=dim)
        edges[dim] = (
            lax.ppermute(last, axis, up),
            lax.ppermute(initial, axis, [(b, a) for a, b in up]),
        )
    done = []
    for _, dim in sides:
        low, high = edges[dim]
        around = [(width, width) if d in done else (0, 0) for d in range(shard.ndim)]
        shard = jnp.concatenate([jnp.pad(low, around), shard, jnp.pad(high, around)], axis=dim)
        done.append(dim)
    return shard


def extended(block, sides, width):
    for axis, dim in sides:
        count = lax.axis_size(axis)
        forward = [(i, i + 1) for i in range(count - 1)]
        backward = [(target, source) for source, target in forward]
        low = lax.ppermute(
            lax.slice_in_dim(block, block.shape[dim] - width, None, axis=dim), axis, forward
        )
        high = lax.ppermute(lax.slice_in_dim(block, 0, width, axis=dim), axis, backward)
        block = jnp.concatenate([low, block, high], axis=dim)
    return block


def over_axes(shard, axes):
    return functools.reduce(lax.psum, axes, shard)


def jacobi_sweep(padded, coefficients, scaled):
    center = padded[:, 1:-1, 1:-1, 1:-1]
    beside = coefficients[0] * (padded[:, 2:, 1:-1, 1:-1] + padded[:, :-2, 1:-1, 1:-1])
    beside = beside + coefficients[1] * (padded[:, 1:-1, 2:, 1:-1] + padded[:, 1:-1, :-2, 1:-1])
    beside = beside + coefficients[2] * (padded[:, 1:-1, 1:-1, 2:] + padded[:, 1:-1, 1:-1, :-2])
    return (1.0 - omega_weight) * center + scaled * beside


def single_sweep(fields, coefficients, scaled):
    padded = with_halo(fields, (("gx", 1), ("gy", 2), (GZ, 3)), 1)
    return jacobi_sweep(padded, coefficients, scaled)


def inside_axis(length, margin, position, count, dim):
    box_shape = [1, 1, 1, 1]
    box_shape[dim] = length + 2 * margin
    global_index = (
        lax.broadcasted_iota(jnp.int32, tuple(box_shape), dim) - margin + position * length
    )
    return ((global_index >= 0) & (global_index < length * count)).astype(jnp.float32)


def inside_box(extent, margin):
    inside = inside_axis(extent[0], margin, lax.axis_index("gx"), lax.axis_size("gx"), 1)
    inside = inside * inside_axis(extent[1], margin, lax.axis_index("gy"), lax.axis_size("gy"), 2)
    inside = inside * inside_axis(extent[2], margin, lax.axis_index(GZ), lax.axis_size(GZ), 3)
    return inside


def masked_sweeps(padded, count, coefficients, scaled, extent):
    for step_index in range(count):
        padded = jacobi_sweep(padded, coefficients, scaled)
        remaining = count - step_index - 1
        if remaining > 0:
            padded = padded * inside_box(extent, remaining)
    return padded


def orthonormal(gram_total, data):
    lower_factor = jnp.linalg.cholesky(gram_total)
    eye_matrix = jnp.eye(gram_total.shape[0], dtype=gram_total.dtype)
    inverse = jax.scipy.linalg.solve_triangular(lower_factor, eye_matrix, lower=True)
    return jnp.einsum("kl,lxyz->kxyz", inverse, data, precision=lax.Precision.HIGHEST)


def local(test_vectors, aniso):
    coefficients = aniso[:, 0].astype(jnp.float32) / aniso[:, 1].astype(jnp.float32)
    scaled = omega_weight / (2.0 * (coefficients[0] + coefficients[1] + coefficients[2]))
    vectors, rows_x, rows_y, rows_z = test_vectors.shape
    extent = (rows_x, rows_y, rows_z)
    fields = test_vectors
    padded = extended(fields, (("gx", 1), ("gy", 2), (GZ, 3)), 2)
    fields = masked_sweeps(padded, 2, coefficients, scaled, extent)
    fields = single_sweep(fields, coefficients, scaled)
    flattened = fields.reshape(vectors, -1)
    gram_part = jnp.dot(flattened, flattened.T, precision=lax.Precision.HIGHEST)
    coarse = fields.reshape(vectors, rows_x // 2, 2, rows_y // 2, 2, rows_z // 2, 2).mean(
        axis=(2, 4, 6)
    )
    coarse_flat = coarse.reshape(vectors, -1)
    coarse_part = jnp.dot(coarse_flat, coarse_flat.T, precision=lax.Precision.HIGHEST)
    gram_total, coarse_gram = (over_axes(gram_part, GX_GY_GZ), over_axes(coarse_part, GX_GY_GZ))
    cell_count = (
        rows_x * rows_y * rows_z * lax.axis_size("gx") * lax.axis_size("gy") * lax.axis_size(GZ)
    )
    gram_total = gram_total / cell_count
    coarse_gram = coarse_gram / (cell_count // 8)
    return (orthonormal(gram_total, fields), orthonormal(coarse_gram, coarse))


def solution(mesh):
    torus = Mesh(
        mesh.devices.reshape(mesh.shape["gx"], mesh.shape["gy"], 4, 2), ("gx", "gy", "gz_0", "gz_1")
    )
    in_specs = (P(None, "gx", "gy", GZ), P())
    out_specs = (P(None, "gx", "gy", GZ), P(None, "gx", "gy", GZ))
    return jax.shard_map(local, mesh=torus, in_specs=in_specs, out_specs=out_specs, check_vma=False)
```

profile of v0, /device:TPU:1, one launch (start us, length us, event | category | flops | bytes accessed | tf_op | source)
XLA Modules:
  0.0 591.9 jit_solution(10206242084911033901)
XLA Ops:
  0.6 1.8 fusion.48
  3.1 4.6 collective-permute-start
  8.3 1.3 collective-permute-start.1
  9.6 19.8 %collective-permute-done = f32[8,2,16,1024]{3,0,2,1:T(8,128)S(1)} collective-permute-done((f32[8,2,16,1024]{3,0,2,1:T(8,128)S(1)}, f32[8,2,16,1024]{3,0,2,1:T(8,128)S(1)}, u32[]{:S(2)}, u32[]{:S(2)}) %collective-permute-start) | collective-permute-done | bytes 1048608 | tf_op jit(solution)/shard_map/ppermute | solution.py:41
  29.5 7.1 %constant_dynamic-update-slice_fusion.1 = f32[8,20,16,1024]{3,0,2,1:T(8,128)S(1)} fusion(f32[8,20,16,1024]{3,0,2,1:T(8,128)S(1)} %constant_dynamic-update-slice_fusion.2, f32[8,16,16,1024]{3,2,1,0:T(8,128)S(1)} %copy-done.2), kind=kLoop, calls=%fused_computation.77 | loop fusion | bytes 16777216
  36.8 4.0 copy-done.1
  40.8 1.7 fusion.44
  42.4 3.3 collective-permute-start.2
  45.7 1.3 collective-permute-start.3
  47.1 1.5 broadcast_multiply_fusion
  48.6 23.9 %collective-permute-done.2 = f32[8,20,2,1024]{3,0,2,1:T(8,128)S(1)} collective-permute-done((f32[8,20,2,1024]{3,0,2,1:T(8,128)}, f32[8,20,2,1024]{3,0,2,1:T(8,128)S(1)}, u32[]{:S(2)}, u32[]{:S(2)}) %collective-permute-start.2) | collective-permute-done | bytes 1310752 | tf_op jit(solution)/shard_map/ppermute | solution.py:41
  72.5 3.8 collective-permute-done.3
  76.3 1.1 copy-done.4
  77.5 5.3 pad_maximum_fusion
  82.8 4.8 copy-done
  89.2 5.9 %collective-permute-start.4 = (f32[8,20,20,2]{2,0,3,1:T(8,128)S(1)}, f32[8,20,20,2]{2,0,3,1:T(8,128)S(1)}, u32[]{:S(2)}, u32[]{:S(2)}) collective-permute-start(f32[8,20,20,2]{2,0,3,1:T(8,128)S(1)} %copy.59), channel_id=1, source_target_pairs={{0,1},{1,2},{2,3},{3,4},{4,5},{5,6},{6,7},{8,9},{9,10},{10,11},{11... | collective-permute-start | bytes 76808 | tf_op jit(solution)/shard_map/ppermute | solution.py:41
  96.2 1.9 collective-permute-start.5
  100.7 1.1 copy.61
  102.9 2.2 copy.62
  105.1 17.8 %concatenate.42 = f32[8,20,20,1028]{3,0,2,1:T(8,128)} concatenate(f32[8,20,20,2]{3,0,2,1:T(8,128)S(1)} %copy.61, f32[8,20,20,1024]{3,0,2,1:T(8,128)} %copy-done, f32[8,20,20,2]{3,0,2,1:T(8,128)} %copy.62), dimensions={3} | concatenate | bytes 26316800 | tf_op jit(solution)/shard_map/concatenate | solution.py:45
  123.0 36.8 %fusion.5 = f32[8,18,18,1026]{3,0,2,1:T(8,128)S(1)} fusion(f32[8,20,20,2]{3,0,2,1:T(8,128)S(1)} %copy.61, f32[8,20,2,1024]{3,0,2,1:T(8,128)} %copy-done.4, f32[8,20,16,1024]{3,0,2,1:T(8,128)} %copy-done.1, f32[8,20,2,1024]{3,0,2,1:T(8,128)} %copy-done.3, f32[8,20,20,2]{3,0,2,1:T(8,128)} %copy.62, f32[8,20,20,1028]{3,0,2,1:T(8,128)} %concatenate.42, ...), kind=kLoop, calls=%fused_computation.7 | loop fusion | flops 47869056 | bytes 78313520 | tf_op jit(solution)/shard_map/mul | solution.py:87
  159.8 16.5 %fusion.24 = f32[8,16,16,1024]{3,0,2,1:T(8,128)} fusion(f32[8,18,18,1026]{3,0,2,1:T(8,128)S(1)} %fusion.5, f32[]{:T(128)} %bitcast.2, f32[]{:T(128)} %bitcast.1, f32[]{:T(128)} %bitcast, f32[]{:T(128)S(6)} %div.32), kind=kLoop, calls=%fused_computation.55 | loop fusion | flops 23068672 | bytes 67108880 | tf_op jit(solution)/shard_map/add | solution.py:58
  176.3 1.3 fusion.47
  178.7 1.3 collective-permute-start.8
  180.0 2.3 fusion.46
  183.4 4.8 collective-permute-start.9
  188.1 1.3 collective-permute-start.6
  189.4 4.8 collective-permute-start.7
  194.2 1.9 fusion.45
  197.0 1.9 collective-permute-start.10
  199.7 2.8 collective-permute-done.10
  202.5 1.9 collective-permute-start.11
  206.6 1.4 copy.66
  208.0 1.4 copy.68
  209.5 36.8 %fusion.14 = f32[8,16,16,1024]{3,0,2,1:T(8,128)} fusion(f32[8,16,16,1]{3,0,2,1:T(8,128)S(1)} %copy.72, f32[8,18,1,1024]{3,0,2,1:T(8,128)S(1)} %pad.14, f32[8,18,1,1024]{3,0,2,1:T(8,128)S(1)} %pad.15, f32[8,1,16,1024]{3,0,2,1:T(8,128)S(1)} %collective-permute-done.6, f32[8,16,16,1024]{3,0,2,1:T(8,128)} %fusion.24, ...), kind=kLoop, calls=%fused_computation.25 | loop fusion | flops 73400320 | bytes 19021840 | tf_op jit(solution)/shard_map/add | solution.py:58
  246.2 65.5 %copy.76 = f32[8,16,16,1024]{0,3,2,1:T(8,128)} copy(f32[8,16,16,1024]{3,0,2,1:T(8,128)} %fusion.14) | data formatting | bytes 16777216 | tf_op jit(solution)/shard_map/add | solution.py:58
  311.8 21.7 %convolution_bitcast_fusion = f32[8,8]{0,1:T(8,128)S(1)} fusion(f32[8,16,16,1024]{3,0,2,1:T(8,128)} %fusion.14), kind=kOutput, calls=%fused_computation.62 | convolution fusion | flops 201326592 | bytes 8388864 | tf_op jit(solution)/shard_map/dot_general | solution.py:108
  333.5 183.6 %reduce_sum.9 = f32[8,8,8,512]{0,3,2,1:T(8,128)} reduce(f32[8,8,2,8,2,512,2]{0,6,5,4,3,2,1:T(2,128)} %bitcast.9, f32[]{:T(128)} %constant.84.clone.1), dimensions={2,4,6}, to_apply=%region_6.9 | reduce | flops 1835008 | bytes 9437188 | tf_op jit(solution)/shard_map/reduce_sum | solution.py:109
  517.1 9.8 %copy.77 = f32[8,8,8,512]{3,2,1,0:T(8,128)S(1)} copy(f32[8,8,8,512]{0,3,2,1:T(8,128)} %reduce_sum.9) | data formatting | bytes 2097152 | tf_op jit(solution)/shard_map/reduce_sum | solution.py:109
  527.1 2.5 convolution_bitcast_fusion.2
  529.6 8.0 %all-reduce.6 = (f32[8,8]{0,1:T(8,128)S(1)}, f32[8,8]{0,1:T(8,128)S(1)}) all-reduce(f32[8,8]{0,1:T(8,128)S(1)} %convolution_bitcast_fusion, f32[8,8]{0,1:T(8,128)S(1)} %convolution_bitcast_fusion.2), channel_id=1, replica_groups=mesh['gx'=4,'gy'=4,'gz_0'=4,'gz_1'=2] {'gx'}, use_global_device_ids=true, to_apply=%region_0.1 | all-reduce | flops 128 | bytes 1024 | tf_op jit(solution)/shard_map/psum | solution.py:50
  537.6 6.9 %all-reduce.5 = (f32[8,8]{0,1:T(8,128)S(1)}, f32[8,8]{0,1:T(8,128)S(1)}) all-reduce(f32[8,8]{0,1:T(8,128)S(1)} %get-tuple-element.16, f32[8,8]{0,1:T(8,128)S(1)} %get-tuple-element.17), channel_id=1, replica_groups=mesh['gx'=4,'gy'=4,'gz_0'=4,'gz_1'=2] {'gy'}, use_global_device_ids=true, to_apply=%region_1.2 | all-reduce | flops 128 | bytes 1024 | tf_op jit(solution)/shard_map/psum | solution.py:50
  544.5 7.4 %all-reduce.4 = (f32[8,8]{0,1:T(8,128)S(1)}, f32[8,8]{0,1:T(8,128)S(1)}) all-reduce(f32[8,8]{0,1:T(8,128)S(1)} %get-tuple-element.14, f32[8,8]{0,1:T(8,128)S(1)} %get-tuple-element.15), channel_id=1, replica_groups=mesh['gx'=4,'gy'=4,'gz_0'=4,'gz_1'=2] {'gz_0'}, use_global_device_ids=true, to_apply=%region_2.3 | all-reduce | flops 128 | bytes 1024 | tf_op jit(solution)/shard_map/psum | solution.py:50
  551.9 10.7 %all-reduce.7 = (f32[8,8]{0,1:T(8,128)S(1)}, f32[8,8]{0,1:T(8,128)S(1)}) all-reduce(f32[8,8]{0,1:T(8,128)S(1)} %get-tuple-element.12, f32[8,8]{0,1:T(8,128)S(1)} %get-tuple-element.13), channel_id=1, replica_groups=mesh['gx'=4,'gy'=4,'gz_0'=4,'gz_1'=2] {'gz_1'}, use_global_device_ids=true, to_apply=%region_3.4 | all-reduce | flops 128 | bytes 1024 | tf_op jit(solution)/shard_map/psum | solution.py:50
  565.6 1.5 fusion.28
  567.1 1.6 copy.85
  571.7 11.5 %fusion.50 = f32[8,16,16,1024]{3,0,2,1:T(8,128)S(1)} fusion(f32[8,8,1,1]{1,0,3,2:T(8,128)S(1)} %convolution_bitcast_fusion.3, f32[8,16,16,1024]{3,0,2,1:T(8,128)} %fusion.14), kind=kOutput, calls=%fused_computation.111 | convolution fusion | flops 201326592 | bytes 16777472 | tf_op jit(solution)/shard_map/kl,lxyz->kxyz/dot_general | solution.py:95
  583.2 8.3 %copy.84 = f32[8,16,16,1024]{3,2,1,0:T(8,128)} copy(f32[8,16,16,1024]{3,0,2,1:T(8,128)S(1)} %fusion.50) | data formatting | bytes 16777216
  (56 shorter events, 18.1 us)
Async XLA Ops:
  0.6 28.9 %copy-start.2 = (f32[8,16,16,1024]{3,2,1,0:T(8,128)S(1)}, f32[8,16,16,1024]{3,2,1,0:T(8,128)}, u32[]{:S(2)}) copy-start(f32[8,16,16,1024]{3,2,1,0:T(8,128)} %param.5) | copy-start | bytes 25165828
  3.1 26.3 %collective-permute-start = (f32[8,2,16,1024]{3,0,2,1:T(8,128)S(1)}, f32[8,2,16,1024]{3,0,2,1:T(8,128)S(1)}, u32[]{:S(2)}, u32[]{:S(2)}) collective-permute-start(f32[8,2,16,1024]{3,0,2,1:T(8,128)S(1)} %copy.97), channel_id=1, source_target_pairs={{0,32},{32,64},{64,96},{1,33},{33,65},{65,97},{2,34},{34,66},{66,9... | collective-permute-start | bytes 3145736 | tf_op jit(solution)/shard_map/ppermute | solution.py:41
  8.3 28.4 %collective-permute-start.1 = (f32[8,2,16,1024]{3,0,2,1:T(8,128)S(1)}, f32[8,2,16,1024]{3,0,2,1:T(8,128)S(1)}, u32[]{:S(2)}, u32[]{:S(2)}) collective-permute-start(f32[8,2,16,1024]{3,0,2,1:T(8,128)S(1)} %copy.98), channel_id=1, source_target_pairs={{32,0},{64,32},{96,64},{33,1},{65,33},{97,65},{34,2},{66,34},{98,6... | collective-permute-start | bytes 3145736 | tf_op jit(solution)/shard_map/ppermute | solution.py:44
  29.5 17.5 %copy-start.5 = (s32[3,2]{0,1:T(2,128)S(1)}, s32[3,2]{0,1:T(2,128)}, u32[]{:S(2)}) copy-start(s32[3,2]{0,1:T(2,128)} %param.6) | copy-start | bytes 76
  36.8 4.0 copy-start.1
  42.4 30.1 %collective-permute-start.2 = (f32[8,20,2,1024]{3,0,2,1:T(8,128)}, f32[8,20,2,1024]{3,0,2,1:T(8,128)S(1)}, u32[]{:S(2)}, u32[]{:S(2)}) collective-permute-start(f32[8,20,2,1024]{3,0,2,1:T(8,128)} %get-tuple-element.22), channel_id=1, source_target_pairs={{0,8},{8,16},{16,24},{1,9},{9,17},{17,25},{2,10},{10,18},{18,26},{... | collective-permute-start | bytes 3932168 | tf_op jit(solution)/shard_map/ppermute | solution.py:41
  45.7 30.6 %collective-permute-start.3 = (f32[8,20,2,1024]{3,0,2,1:T(8,128)}, f32[8,20,2,1024]{3,0,2,1:T(8,128)S(1)}, u32[]{:S(2)}, u32[]{:S(2)}) collective-permute-start(f32[8,20,2,1024]{3,0,2,1:T(8,128)} %get-tuple-element.23), channel_id=1, source_target_pairs={{8,0},{16,8},{24,16},{9,1},{17,9},{25,17},{10,2},{18,10},{26,18},{... | collective-permute-start | bytes 3932168 | tf_op jit(solution)/shard_map/ppermute | solution.py:44
  72.5 3.8 copy-start.3
  76.3 1.1 copy-start.4
  82.7 4.8 copy-start
  89.2 11.5 %collective-permute-start.4 = (f32[8,20,20,2]{2,0,3,1:T(8,128)S(1)}, f32[8,20,20,2]{2,0,3,1:T(8,128)S(1)}, u32[]{:S(2)}, u32[]{:S(2)}) collective-permute-start(f32[8,20,20,2]{2,0,3,1:T(8,128)S(1)} %copy.59), channel_id=1, source_target_pairs={{0,1},{1,2},{2,3},{3,4},{4,5},{5,6},{6,7},{8,9},{9,10},{10,11},{11... | collective-permute-start | bytes 76808 | tf_op jit(solution)/shard_map/ppermute | solution.py:41
  96.2 6.6 %collective-permute-start.5 = (f32[8,20,20,2]{2,0,3,1:T(8,128)S(1)}, f32[8,20,20,2]{2,0,3,1:T(8,128)S(1)}, u32[]{:S(2)}, u32[]{:S(2)}) collective-permute-start(f32[8,20,20,2]{2,0,3,1:T(8,128)S(1)} %copy.60), channel_id=1, source_target_pairs={{1,0},{2,1},{3,2},{4,3},{5,4},{6,5},{7,6},{9,8},{10,9},{11,10},{12... | collective-permute-start | bytes 76808 | tf_op jit(solution)/shard_map/ppermute | solution.py:44
  178.7 27.9 %collective-permute-start.8 = (f32[8,16,1,1024]{3,1,2,0:T(8,128)}, f32[8,16,1,1024]{3,1,2,0:T(8,128)}, u32[]{:S(2)}, u32[]{:S(2)}) collective-permute-start(f32[8,16,1,1024]{3,1,2,0:T(8,128)} %copy.65), channel_id=1, source_target_pairs={{8,0},{16,8},{24,16},{9,1},{17,9},{25,17},{10,2},{18,10},{26,18},{... | collective-permute-start | bytes 1572872 | tf_op jit(solution)/shard_map/ppermute | solution.py:25
  183.4 24.7 %collective-permute-start.9 = (f32[8,16,1,1024]{3,1,2,0:T(8,128)}, f32[8,16,1,1024]{3,1,2,0:T(8,128)}, u32[]{:S(2)}, u32[]{:S(2)}) collective-permute-start(f32[8,16,1,1024]{3,1,2,0:T(8,128)} %copy.67), channel_id=1, source_target_pairs={{0,8},{8,16},{16,24},{1,9},{9,17},{17,25},{2,10},{10,18},{18,26},{... | collective-permute-start | bytes 1572872 | tf_op jit(solution)/shard_map/ppermute | solution.py:24
  188.1 21.3 %collective-permute-start.6 = (f32[8,1,16,1024]{3,0,2,1:T(8,128)}, f32[8,1,16,1024]{3,0,2,1:T(8,128)S(1)}, u32[]{:S(2)}, u32[]{:S(2)}) collective-permute-start(f32[8,1,16,1024]{3,0,2,1:T(8,128)} %get-tuple-element.27), channel_id=1, source_target_pairs={{32,0},{64,32},{96,64},{33,1},{65,33},{97,65},{34,2},{66,34},{98,6... | collective-permute-start | bytes 1572872 | tf_op jit(solution)/shard_map/ppermute | solution.py:25
  189.4 20.0 %collective-permute-start.7 = (f32[8,1,16,1024]{3,0,2,1:T(8,128)}, f32[8,1,16,1024]{3,0,2,1:T(8,128)S(1)}, u32[]{:S(2)}, u32[]{:S(2)}) collective-permute-start(f32[8,1,16,1024]{3,0,2,1:T(8,128)} %get-tuple-element.26), channel_id=1, source_target_pairs={{0,32},{32,64},{64,96},{1,33},{33,65},{65,97},{2,34},{34,66},{66,9... | collective-permute-start | bytes 1572872 | tf_op jit(solution)/shard_map/ppermute | solution.py:24
  197.0 5.6 collective-permute-start.10
  202.5 3.2 collective-permute-start.11
where the time goes:
time: 603 us; the launch traced here: 592 us
  other arithmetic  286 us (47%)
  local copies, waits for them, and re-layouts  146 us (24%)
  waiting for transfers between devices  51.9 us (9%)
  matrix products  37.6 us (6%)
  starting transfers between devices  34.2 us (6%)
  blocking collectives  33 us (5%)
    reduce_sum x1, other arithmetic, local(): fields.reshape(vectors, rows_x // 2, 2, rows_y // 2, 2, rows_z // 2, 2)  184 us
    add x1, local copies, waits for them, and re-layouts, jacobi_sweep(): return (1.0 - omega_weight) * center + scaled * beside  65.5 us
    add x2, other arithmetic, jacobi_sweep(): return (1.0 - omega_weight) * center + scaled * beside  53.3 us
    ppermute x3, waiting for transfers between devices, extended(): lax.ppermute(lax.slice_in_dim(block, block.shape[dim] - width, None, axis...  43.7 us
    mul x1, other arithmetic, masked_sweeps(): padded = padded * inside_box(extent, remaining)  36.8 us
    psum x4, blocking collectives, over_axes(): return functools.reduce(lax.psum, axes, shard)  33 us
    unnamed x18, local copies, waits for them, and re-layouts  28.2 us
    dot_general x1, matrix products, local(): gram_part = jnp.dot(flattened, flattened.T, precision=lax.Precision.HIGHEST)  21.7 us
  transfers between devices with their start and end apart: 12, of which 6 were waited for; matrix products, arithmetic and copies ran while one was open for 4% of the time, Pallas kernels for 0%

commit v1 on v0

v1 whole, which is shorter than its diff:
```python
import functools

import jax
import jax.numpy as jnp
from jax import lax
from jax.experimental import pallas as pl
from jax.experimental.pallas import tpu as pltpu
from jax.sharding import PartitionSpec as P

MESH = pl.DeviceIdType.MESH
omega_weight = 2.0 / 3.0
K = 8
SWEEPS = 3
LANES = 128
AXES = ("gx", "gy", "gz")


def sweep_kernel(
    sizes,
    aniso_ref,
    in_ref,
    fields_ref,
    coarse_ref,
    gram_ref,
    state,
    ysend,
    yrecv,
    pairs,
    quarter,
    fine_acc,
    coarse_acc,
    gather_z,
    gather_y,
    gather_x,
    load_sem,
    send_sem,
    recv_sem,
    gsend_sem,
    grecv_sem,
):
    rows_x, rows_y, blocks = (in_ref.shape[1], in_ref.shape[2], in_ref.shape[3] // LANES)
    area = blocks * rows_y
    position = {axis: lax.axis_index(axis) for axis in AXES}

    def load(k, block):
        return pltpu.make_async_copy(
            in_ref.at[k, :, :, pl.ds(block * LANES, LANES)],
            state.at[0, k, pl.ds(1, rows_x), pl.ds((block + 1) * rows_y, rows_y), :],
            load_sem.at[k, block],
        )

    def start_loads(k, carry):
        for block in range(blocks):
            load(k, block).start()
        return carry

    lax.fori_loop(0, K, start_loads, 0)

    barrier = pltpu.get_barrier_semaphore()
    peers = 0
    for axis in AXES:
        for offset in range(1, sizes[axis]):
            peer = lax.rem(position[axis] + offset, sizes[axis])
            pl.semaphore_signal(barrier, inc=1, device_id={axis: peer}, device_id_type=MESH)
            peers += 1

    def as_float(d, j):
        return jnp.full((8, LANES), aniso_ref[d, j], jnp.int32).astype(jnp.float32)

    coefficients = [as_float(d, 0) / as_float(d, 1) for d in range(3)]
    scaled = omega_weight / (2.0 * (coefficients[0] + coefficients[1] + coefficients[2]))
    weights = [scaled * c for c in coefficients]
    keep = 1.0 - omega_weight

    lane = lax.broadcasted_iota(jnp.int32, (8, LANES), 1)
    row = lax.broadcasted_iota(jnp.int32, (8, LANES), 0)

    def face(s, k, direction):
        b = s % 2
        axis, side = AXES[direction // 2], direction % 2
        peer = position[axis] + (1 if side else -1)
        if axis == "gx":
            source = state.at[b, k, rows_x if side else 1, pl.ds(rows_y, area), :]
            target = state.at[b, k, 0 if side else rows_x + 1, pl.ds(rows_y, area), :]
        elif axis == "gy":
            source = ysend.at[s, side, k]
            target = yrecv.at[s, side, k]
        else:
            from_row = blocks * rows_y if side else rows_y
            to_row = 0 if side else (blocks + 1) * rows_y
            source = state.at[b, k, pl.ds(1, rows_x), pl.ds(from_row, rows_y), :]
            target = state.at[b, k, pl.ds(1, rows_x), pl.ds(to_row, rows_y), :]
        return pltpu.make_async_remote_copy(
            src_ref=source,
            dst_ref=target,
            send_sem=send_sem.at[direction, s, k],
            recv_sem=recv_sem.at[direction, s, k],
            device_id={axis: peer},
            device_id_type=MESH,
        )

    def can_send(direction):
        axis, side = AXES[direction // 2], direction % 2
        return position[axis] < sizes[axis] - 1 if side else position[axis] > 0

    def can_receive(direction):
        return can_send(direction ^ 1)

    def send(s, k):
        b = s % 2

        def pack(x, carry):
            for side in range(2):
                first = rows_y + (rows_y - 1 if side else 0)
                ysend[s, side, k, x] = state[b, k, x + 1, pl.ds(first, blocks, stride=rows_y), :]
            return carry

        lax.fori_loop(0, rows_x, pack, 0, unroll=4)
        for direction in range(6):

            @pl.when(can_send(direction))
            def _():
                face(s, k, direction).start()

    def wait_faces(s, k):
        for direction in range(6):

            @pl.when(can_receive(direction))
            def _():
                face(s, k, direction).wait_recv()

    def wait_sent(s, k):
        for direction in range(6):

            @pl.when(can_send(direction))
            def _():
                face(s, k, direction).wait_send()

    zero = jnp.zeros((8, LANES), jnp.float32)

    def clear(direction):
        axis, side = AXES[direction // 2], direction % 2

        def clear_one(k, carry):
            if axis == "gx":
                plane = 0 if side else rows_x + 1
                for b in range(2):
                    for r in range(0, area, 8):
                        state[b, k, plane, rows_y + r : rows_y + r + 8, :] = zero
            elif axis == "gy":
                for s in range(SWEEPS):
                    for x in range(rows_x):
                        yrecv[s, side, k, x] = zero
            else:
                first = 0 if side else (blocks + 1) * rows_y
                for b in range(2):
                    for x in range(rows_x):
                        for r in range(0, rows_y, 8):
                            state[b, k, x + 1, first + r : first + r + 8, :] = zero
            return carry

        lax.fori_loop(0, K, clear_one, 0)

    for direction in range(6):

        @pl.when(jnp.logical_not(can_receive(direction)))
        def _():
            clear(direction)

    pl.semaphore_wait(barrier, peers)

    def first_sends(k, carry):
        for block in range(blocks):
            load(k, block).wait()
        send(0, k)
        return carry

    lax.fori_loop(0, K, first_sends, 0)

    def plane_sweep(s, k, x, store):
        b = s % 2
        for y in range(0, rows_y, 8):
            center = [
                state[b, k, x, n * rows_y + y : n * rows_y + y + 8, :] for n in range(blocks + 2)
            ]
            for n in range(1, blocks + 1):
                r = n * rows_y + y
                beside_x = state[b, k, x - 1, r : r + 8, :] + state[b, k, x + 1, r : r + 8, :]
                low = state[b, k, x, r - 1 : r + 7, :]
                high = state[b, k, x, r + 1 : r + 9, :]
                if y == 0:
                    edge = jnp.broadcast_to(yrecv[s, 1, k, x - 1, n - 1 : n, :], (8, LANES))
                    low = jnp.where(row == 0, edge, low)
                if y == rows_y - 8:
                    edge = jnp.broadcast_to(yrecv[s, 0, k, x - 1, n - 1 : n, :], (8, LANES))
                    high = jnp.where(row == 7, edge, high)
                left = pltpu.roll(jnp.where(lane == LANES - 1, center[n - 1], center[n]), 1, 1)
                right = pltpu.roll(jnp.where(lane == 0, center[n + 1], center[n]), LANES - 1, 1)
                value = keep * center[n] + weights[0] * beside_x
                value = value + weights[1] * (low + high)
                value = value + weights[2] * (left + right)
                store(n, y, value)

    for s in range(SWEEPS - 1):

        def one_vector(k, carry, s=s):
            wait_faces(s, k)
            if s > 0:
                wait_sent(s - 1, k)
            b = (s + 1) % 2

            def one_plane(x, carry):
                def store(n, y, value):
                    r = n * rows_y + y
                    state[b, k, x, r : r + 8, :] = value

                plane_sweep(s, k, x, store)
                return carry

            lax.fori_loop(1, rows_x + 1, one_plane, 0)
            send(s + 1, k)
            return carry

        lax.fori_loop(0, K, one_vector, 0)

    pick_row = lax.broadcasted_iota(jnp.int32, (2 * LANES, LANES), 0)
    pick_col = lax.broadcasted_iota(jnp.int32, (2 * LANES, LANES), 1)
    pick = jnp.where(pick_row // 2 == pick_col, 0.125, 0.0).astype(jnp.bfloat16)
    half_x, half_y = rows_x // 2, rows_y // 2
    s = SWEEPS - 1
    for k in range(K):
        wait_faces(s, k)

        def last_plane(x, sums):
            sums = list(sums)

            def store(n, y, value):
                window = (x - 1, slice(y, y + 8), slice((n - 1) * LANES, n * LANES))
                fields_ref[(k, *window)] = value
                for other in range(k):
                    sums[other] = sums[other] + value * fields_ref[(other, *window)]
                sums[k] = sums[k] + value * value

            plane_sweep(s, k, x, store)
            return tuple(sums)

        sums = lax.fori_loop(1, rows_x + 1, last_plane, (zero,) * (k + 1))
        for other in range(k + 1):
            fine_acc[k, other] = sums[other]

        def aggregate(i, carry):
            for n in range(blocks):
                columns = slice(n * LANES, (n + 1) * LANES)
                for y in range(0, rows_y, 8):
                    pairs[n, y : y + 8, :] = (
                        fields_ref[k, 2 * i, y : y + 8, columns]
                        + fields_ref[k, 2 * i + 1, y : y + 8, columns]
                    )
            for n in range(blocks):
                columns = slice(n * LANES, (n + 1) * LANES)
                quarter[i, :, columns] = (
                    pairs[n, pl.ds(0, half_y, stride=2), :]
                    + pairs[n, pl.ds(1, half_y, stride=2), :]
                )
            return carry

        lax.fori_loop(0, half_x, aggregate, 0)
        for n in range(0, blocks, 2):
            whole = quarter[:, :, n * LANES : (n + 2) * LANES]
            whole = whole.reshape(half_x * half_y, 2 * LANES)
            total = None
            for _ in range(3):
                part = whole.astype(jnp.bfloat16)
                whole = whole - part.astype(jnp.float32)
                product = jnp.dot(part, pick, preferred_element_type=jnp.float32)
                total = product if total is None else total + product
            columns = slice(n // 2 * LANES, (n // 2 + 1) * LANES)
            coarse_ref[k, :, :, columns] = total.reshape(half_x, half_y, LANES)

        def coarse_products(i, sums):
            sums = list(sums)
            for n in range(blocks // 2):
                columns = slice(n * LANES, (n + 1) * LANES)
                value = coarse_ref[k, i, :, columns]
                for other in range(k):
                    sums[other] = sums[other] + value * coarse_ref[other, i, :, columns]
                sums[k] = sums[k] + value * value
            return tuple(sums)

        sums = lax.fori_loop(0, half_x, coarse_products, (zero,) * (k + 1))
        for other in range(k + 1):
            coarse_acc[k, other] = sums[other]

    part = zero
    for which, acc in enumerate((fine_acc, coarse_acc)):
        for k in range(K):
            stacked = zero
            for other in range(K):
                tile = acc[max(k, other), min(k, other)]
                summed = jnp.sum(tile, axis=0, keepdims=True)
                stacked = jnp.where(row == other, summed, stacked)
            column = jnp.sum(stacked, axis=1, keepdims=True)
            part = jnp.where(lane == which * K + k, column, part)

    for number, (axis, slots) in enumerate((("gz", gather_z), ("gy", gather_y), ("gx", gather_x))):
        count = sizes[axis]
        me = position[axis]
        slots[me] = part

        def exchange(offset, axis=axis, slots=slots, me=me, count=count, number=number):
            return pltpu.make_async_remote_copy(
                src_ref=slots.at[me],
                dst_ref=slots.at[me],
                send_sem=gsend_sem.at[number, offset],
                recv_sem=grecv_sem.at[number, offset],
                device_id={axis: lax.rem(me + offset, count)},
                device_id_type=MESH,
            )

        def arrival(offset, axis=axis, slots=slots, me=me, count=count, number=number):
            source = lax.rem(me + count - offset, count)
            return pltpu.make_async_remote_copy(
                src_ref=slots.at[source],
                dst_ref=slots.at[source],
                send_sem=gsend_sem.at[number, offset],
                recv_sem=grecv_sem.at[number, offset],
                device_id={axis: source},
                device_id_type=MESH,
            )

        for offset in range(1, count):
            exchange(offset).start()
        for offset in range(1, count):
            arrival(offset).wait_recv()
        part = slots[0]
        for slot in range(1, count):
            part = part + slots[slot]
        for offset in range(1, count):
            exchange(offset).wait_send()
    gram_ref[...] = part

    def finish(k, carry):
        for s in range(SWEEPS - 2, SWEEPS):
            wait_sent(s, k)
        return carry

    lax.fori_loop(0, K, finish, 0)


def inverse_factor(gram, lane, row):
    work = jnp.where(lane < K, gram, 0.0) + jnp.where(lane == row + K, 1.0, 0.0)
    for j in range(K):
        pivot_row = jnp.broadcast_to(work[j : j + 1, :], work.shape)
        column = jnp.broadcast_to(work[:, j : j + 1], work.shape)
        pivot = jnp.broadcast_to(pivot_row[:, j : j + 1], work.shape)
        factor = jnp.where(row > j, column / pivot, 0.0)
        work = work - factor * pivot_row
    pivots = jnp.sum(jnp.where(lane == row, work, 0.0), axis=1, keepdims=True)
    scale = 1.0 / jnp.sqrt(pivots)
    return pltpu.roll(work * scale, LANES - K, 1)


def basis_kernel(
    cells,
    gram_ref,
    fields_ref,
    coarse_ref,
    basis_ref,
    coarse_basis_ref,
    stage,
    coarse_stage,
    table,
    out_sem,
    coarse_sem,
):
    rows_x, rows_y, blocks = (
        fields_ref.shape[1],
        fields_ref.shape[2],
        fields_ref.shape[3] // LANES,
    )
    lane = lax.broadcasted_iota(jnp.int32, (8, LANES), 1)
    row = lax.broadcasted_iota(jnp.int32, (8, LANES), 0)
    gram = gram_ref[...]
    fine = inverse_factor(gram / cells, lane, row)
    rest = inverse_factor(pltpu.roll(gram, LANES - K, 1) / (cells // 8), lane, row)
    for which, inverse in enumerate((fine, rest)):
        for other in range(K):
            table[which, other] = jnp.broadcast_to(inverse[:, other : other + 1], (8, LANES))

    def combine(which, windows, source, target):
        loaded = [[source(other, w) for w in windows] for other in range(K)]
        for k in range(K):
            totals = None
            for other in range(k + 1):
                weight = jnp.broadcast_to(table[which, other, k : k + 1, :], (8, LANES))
                products = [weight * value for value in loaded[other]]
                totals = (
                    products if totals is None else [t + p for t, p in zip(totals, products)]
                )
            for w, total in zip(windows, totals):
                target(k, w, total)

    def put(x):
        return pltpu.make_async_copy(stage.at[x], basis_ref.at[:, x], out_sem.at[x])

    def one_plane(x, carry):
        def source(k, w):
            return fields_ref[k, x, w[0] : w[0] + 8, w[1] * LANES : (w[1] + 1) * LANES]

        def target(k, w, value):
            stage[x, k, w[0] : w[0] + 8, w[1] * LANES : (w[1] + 1) * LANES] = value

        windows = [(y, n) for y in range(0, rows_y, 8) for n in range(blocks)]
        for first in range(0, len(windows), 4):
            combine(0, windows[first : first + 4], source, target)
        put(x).start()
        return carry

    lax.fori_loop(0, rows_x, one_plane, 0)

    def one_coarse(x, carry):
        def source(k, n):
            return coarse_ref[k, x, :, n * LANES : (n + 1) * LANES]

        def target(k, n, value):
            coarse_stage[k, x, :, n * LANES : (n + 1) * LANES] = value

        combine(1, list(range(blocks // 2)), source, target)
        return carry

    lax.fori_loop(0, rows_x // 2, one_coarse, 0)
    out = pltpu.make_async_copy(coarse_stage, coarse_basis_ref, coarse_sem)
    out.start()

    def drain(x, carry):
        put(x).wait()
        return carry

    lax.fori_loop(0, rows_x, drain, 0)
    out.wait()


def local(sizes, test_vectors, aniso):
    vectors, rows_x, rows_y, rows_z = test_vectors.shape
    blocks = rows_z // LANES
    half = (vectors, rows_x // 2, rows_y // 2, rows_z // 2)
    f32 = jnp.float32
    hbm = pl.BlockSpec(memory_space=pltpu.HBM)
    smem = pl.BlockSpec(memory_space=pltpu.SMEM)
    vmem = pl.BlockSpec(memory_space=pltpu.VMEM)
    longest = max(sizes.values())
    fields, coarse, gram = pl.pallas_call(
        functools.partial(sweep_kernel, sizes),
        out_shape=(
            pltpu.VMEM(test_vectors.shape, f32),
            pltpu.VMEM(half, f32),
            pltpu.VMEM((8, LANES), f32),
        ),
        in_specs=[smem, hbm],
        out_specs=(vmem, vmem, vmem),
        scratch_shapes=[
            pltpu.VMEM((2, vectors, rows_x + 2, (blocks + 2) * rows_y, LANES), f32),
            pltpu.VMEM((SWEEPS, 2, vectors, rows_x, blocks, LANES), f32),
            pltpu.VMEM((SWEEPS, 2, vectors, rows_x, blocks, LANES), f32),
            pltpu.VMEM((blocks, rows_y, LANES), f32),
            pltpu.VMEM((rows_x // 2, rows_y // 2, rows_z), f32),
            pltpu.VMEM((vectors, vectors, 8, LANES), f32),
            pltpu.VMEM((vectors, vectors, 8, LANES), f32),
            pltpu.VMEM((sizes["gz"], 8, LANES), f32),
            pltpu.VMEM((sizes["gy"], 8, LANES), f32),
            pltpu.VMEM((sizes["gx"], 8, LANES), f32),
            pltpu.SemaphoreType.DMA((vectors, blocks)),
            pltpu.SemaphoreType.DMA((6, SWEEPS, vectors)),
            pltpu.SemaphoreType.DMA((6, SWEEPS, vectors)),
            pltpu.SemaphoreType.DMA((3, longest)),
            pltpu.SemaphoreType.DMA((3, longest)),
        ],
        compiler_params=pltpu.CompilerParams(
            collective_id=0, has_side_effects=True, vmem_limit_bytes=44 * 1024 * 1024
        ),
        name="sweeps",
    )(aniso, test_vectors)
    cells = float(rows_x * rows_y * rows_z * sizes["gx"] * sizes["gy"] * sizes["gz"])
    return pl.pallas_call(
        functools.partial(basis_kernel, cells),
        out_shape=(
            jax.ShapeDtypeStruct(test_vectors.shape, f32),
            jax.ShapeDtypeStruct(half, f32),
        ),
        in_specs=[vmem, vmem, vmem],
        out_specs=(hbm, hbm),
        scratch_shapes=[
            pltpu.VMEM((rows_x, vectors, rows_y, rows_z), f32),
            pltpu.VMEM(half, f32),
            pltpu.VMEM((2, vectors, 8, LANES), f32),
            pltpu.SemaphoreType.DMA((rows_x,)),
            pltpu.SemaphoreType.DMA(()),
        ],
        compiler_params=pltpu.CompilerParams(vmem_limit_bytes=24 * 1024 * 1024),
        name="basis",
    )(gram, fields, coarse)


def solution(mesh):
    sizes = {axis: mesh.shape[axis] for axis in AXES}
    spec = P(None, "gx", "gy", "gz")
    return jax.shard_map(
        functools.partial(local, sizes),
        mesh=mesh,
        in_specs=(spec, P()),
        out_specs=(spec, spec),
        check_vma=False,
    )
```

time: 603 us -> 98.5 us (0.16); the launches traced: 592 us -> 97.7 us
  other arithmetic: 286 us -> 0 us
  local copies, waits for them, and re-layouts: 146 us -> 0.77 us
  Pallas kernels: 0 us -> 96.3 us
  waiting for transfers between devices: 51.9 us -> 0 us
  matrix products: 37.6 us -> 0 us
  starting transfers between devices: 34.2 us -> 0 us
  blocking collectives: 33 us -> 0 us
    reduce_sum x1 -> x0, other arithmetic: 184 us -> none  [local(): fields.reshape(vectors, rows_x // 2, 2, rows_y // 2, 2, rows_z // 2, 2)]
    pallas_call x0 -> x2, Pallas kernels: none -> 96.3 us  [the longest x1 90.5 us: local(): pl.pallas_call(functools.partial(sweep_kernel, sizes), out_shape=(pltpu.V...]
    add x1 -> x0, local copies, waits for them, and re-layouts: 65.5 us -> none  [jacobi_sweep(): return (1.0 - omega_weight) * center + scaled * beside]
    add x2 -> x0, other arithmetic: 53.3 us -> none  [jacobi_sweep(): return (1.0 - omega_weight) * center + scaled * beside]
    ppermute x12 -> x0, waiting for transfers between devices: 51.9 us -> none  [the longest x3 43.7 us: extended(): lax.ppermute(lax.slice_in_dim(block, block.shape[dim] - width, None, axis...]
    mul x3 -> x0, other arithmetic: 38.4 us -> none  [the longest x1 36.8 us: masked_sweeps(): padded = padded * inside_box(extent, remaining)]
    dot_general x4 -> x0, matrix products: 37.2 us -> none  [the longest x1 21.7 us: local(): gram_part = jnp.dot(flattened, flattened.T, precision=lax.Precision.HIGHEST)]
    ppermute x12 -> x0, starting transfers between devices: 34.2 us -> none  [the longest x3 13.8 us: extended(): lax.ppermute(lax.slice_in_dim(block, block.shape[dim] - width, None, axis...]
  transfers between devices with their start and end apart: 12 -> 0, of which waited for: 6 -> 0; matrix products, arithmetic and copies ran while one was open for 4% -> 0% of each run, Pallas kernels for 0% -> 0%
where the time goes in v1:
time: 98.5 us; the launch traced here: 97.7 us
  Pallas kernels  96.3 us (98%)
    pallas_call x1, Pallas kernels, local(): pl.pallas_call(functools.partial(sweep_kernel, sizes), out_shape=(pltpu.V...  90.5 us
    pallas_call x1, Pallas kernels, local(): pl.pallas_call(functools.partial(basis_kernel, cells), out_shape=(jax.Sha...  5.75 us

profile of v1, /device:TPU:1, one launch (start us, length us, event | category | flops | bytes accessed | tf_op | source)
XLA Modules:
  0.0 97.7 jit_solution(10215121341122920336)
XLA Ops:
  0.6 0.8 copy.4.aniso_ref
  1.4 90.5 %sweeps.1 = (f32[8,16,16,1024]{3,2,1,0:T(8,128)S(1)}, f32[8,8,8,512]{3,2,1,0:T(8,128)S(1)}, f32[8,128]{1,0:T(8,128)S(1)}) custom-call(s32[3,2]{1,0:T(4,128)S(1)} %copy.4.aniso_ref, f32[8,16,16,1024]{3,2,1,0:T(8,128)} %in_ref.1), custom_call_target="tpu_custom_call" | custom-call | tf_op jit(solution)/shard_map/sweeps/pallas_call | solution.py:452
  91.9 5.8 %basis.1 = (f32[8,16,16,1024]{3,2,1,0:T(8,128)}, f32[8,8,8,512]{3,2,1,0:T(8,128)}) custom-call(f32[8,128]{1,0:T(8,128)S(1)} %get-tuple-element.5.gram_ref, f32[8,16,16,1024]{3,2,1,0:T(8,128)S(1)} %get-tuple-element.6.fields_ref, f32[8,8,8,512]{3,2,1,0:T(8,128)S(1)} %get-tuple-element.7.coarse_ref), custom_call_target="tpu_custom_call" | custom-call | tf_op jit(solution)/shard_map/basis/pallas_call | solution.py:484

commit v2 on v1

--- a/solution.py
+++ b/solution.py
@@ -22,11 +22,11 @@
     fields_ref,
     coarse_ref,
     gram_ref,
-    state,
+    even_state,
+    odd_state,
     ysend,
     yrecv,
     pairs,
-    quarter,
     fine_acc,
     coarse_acc,
     gather_z,
@@ -40,12 +40,13 @@
 ):
     rows_x, rows_y, blocks = (in_ref.shape[1], in_ref.shape[2], in_ref.shape[3] // LANES)
     area = blocks * rows_y
+    states = (even_state, odd_state)
     position = {axis: lax.axis_index(axis) for axis in AXES}
 
     def load(k, block):
         return pltpu.make_async_copy(
             in_ref.at[k, :, :, pl.ds(block * LANES, LANES)],
-            state.at[0, k, pl.ds(1, rows_x), pl.ds((block + 1) * rows_y, rows_y), :],
+            even_state.at[k, pl.ds(1, rows_x), pl.ds((block + 1) * rows_y, rows_y), :],
             load_sem.at[k, block],
         )
 
@@ -76,20 +77,20 @@
     row = lax.broadcasted_iota(jnp.int32, (8, LANES), 0)
 
     def face(s, k, direction):
-        b = s % 2
+        state = states[s % 2]
         axis, side = AXES[direction // 2], direction % 2
         peer = position[axis] + (1 if side else -1)
         if axis == "gx":
-            source = state.at[b, k, rows_x if side else 1, pl.ds(rows_y, area), :]
-            target = state.at[b, k, 0 if side else rows_x + 1, pl.ds(rows_y, area), :]
+            source = state.at[k, rows_x if side else 1, pl.ds(rows_y, area), :]
+            target = state.at[k, 0 if side else rows_x + 1, pl.ds(rows_y, area), :]
         elif axis == "gy":
             source = ysend.at[s, side, k]
             target = yrecv.at[s, side, k]
         else:
             from_row = blocks * rows_y if side else rows_y
             to_row = 0 if side else (blocks + 1) * rows_y
-            source = state.at[b, k, pl.ds(1, rows_x), pl.ds(from_row, rows_y), :]
-            target = state.at[b, k, pl.ds(1, rows_x), pl.ds(to_row, rows_y), :]
+            source = state.at[k, pl.ds(1, rows_x), pl.ds(from_row, rows_y), :]
+            target = state.at[k, pl.ds(1, rows_x), pl.ds(to_row, rows_y), :]
         return pltpu.make_async_remote_copy(
             src_ref=source,
             dst_ref=target,
@@ -107,12 +108,12 @@
         return can_send(direction ^ 1)
 
     def send(s, k):
-        b = s % 2
+        state = states[s % 2]
 
         def pack(x, carry):
             for side in range(2):
                 first = rows_y + (rows_y - 1 if side else 0)
-                ysend[s, side, k, x] = state[b, k, x + 1, pl.ds(first, blocks, stride=rows_y), :]
+                ysend[s, side, k, x] = state[k, x + 1, pl.ds(first, blocks, stride=rows_y), :]
             return carry
 
         lax.fori_loop(0, rows_x, pack, 0, unroll=4)
@@ -144,19 +145,19 @@
         def clear_one(k, carry):
             if axis == "gx":
                 plane = 0 if side else rows_x + 1
-                for b in range(2):
+                for state in states:
                     for r in range(0, area, 8):
-                        state[b, k, plane, rows_y + r : rows_y + r + 8, :] = zero
+                        state[k, plane, rows_y + r : rows_y + r + 8, :] = zero
             elif axis == "gy":
                 for s in range(SWEEPS):
                     for x in range(rows_x):
                         yrecv[s, side, k, x] = zero
             else:
                 first = 0 if side else (blocks + 1) * rows_y
-                for b in range(2):
+                for state in states:
                     for x in range(rows_x):
                         for r in range(0, rows_y, 8):
-                            state[b, k, x + 1, first + r : first + r + 8, :] = zero
+                            state[k, x + 1, first + r : first + r + 8, :] = zero
             return carry
 
         lax.fori_loop(0, K, clear_one, 0)
@@ -178,16 +179,16 @@
     lax.fori_loop(0, K, first_sends, 0)
 
     def plane_sweep(s, k, x, store):
-        b = s % 2
+        state = states[s % 2]
         for y in range(0, rows_y, 8):
             center = [
-                state[b, k, x, n * rows_y + y : n * rows_y + y + 8, :] for n in range(blocks + 2)
+                state[k, x, n * rows_y + y : n * rows_y + y + 8, :] for n in range(blocks + 2)
             ]
             for n in range(1, blocks + 1):
                 r = n * rows_y + y
-                beside_x = state[b, k, x - 1, r : r + 8, :] + state[b, k, x + 1, r : r + 8, :]
-                low = state[b, k, x, r - 1 : r + 7, :]
-                high = state[b, k, x, r + 1 : r + 9, :]
+                beside_x = state[k, x - 1, r : r + 8, :] + state[k, x + 1, r : r + 8, :]
+                low = state[k, x, r - 1 : r + 7, :]
+                high = state[k, x, r + 1 : r + 9, :]
                 if y == 0:
                     edge = jnp.broadcast_to(yrecv[s, 1, k, x - 1, n - 1 : n, :], (8, LANES))
                     low = jnp.where(row == 0, edge, low)
@@ -207,89 +208,66 @@
             wait_faces(s, k)
             if s > 0:
                 wait_sent(s - 1, k)
-            b = (s + 1) % 2
+            after = states[(s + 1) % 2]
 
             def one_plane(x, carry):
                 def store(n, y, value):
                     r = n * rows_y + y
-                    state[b, k, x, r : r + 8, :] = value
+                    after[k, x, r : r + 8, :] = value
 
                 plane_sweep(s, k, x, store)
                 return carry
 
-            lax.fori_loop(1, rows_x + 1, one_plane, 0)
+            lax.fori_loop(1, rows_x + 1, one_plane, 0, unroll=4)
             send(s + 1, k)
             return carry
 
         lax.fori_loop(0, K, one_vector, 0)
 
-    pick_row = lax.broadcasted_iota(jnp.int32, (2 * LANES, LANES), 0)
-    pick_col = lax.broadcasted_iota(jnp.int32, (2 * LANES, LANES), 1)
-    pick = jnp.where(pick_row // 2 == pick_col, 0.125, 0.0).astype(jnp.bfloat16)
     half_x, half_y = rows_x // 2, rows_y // 2
+    compact = lax.rem(2 * lane, LANES)
     s = SWEEPS - 1
     for k in range(K):
         wait_faces(s, k)
 
-        def last_plane(x, sums):
-            sums = list(sums)
-
-            def store(n, y, value):
-                window = (x - 1, slice(y, y + 8), slice((n - 1) * LANES, n * LANES))
-                fields_ref[(k, *window)] = value
-                for other in range(k):
-                    sums[other] = sums[other] + value * fields_ref[(other, *window)]
-                sums[k] = sums[k] + value * value
-
-            plane_sweep(s, k, x, store)
-            return tuple(sums)
-
-        sums = lax.fori_loop(1, rows_x + 1, last_plane, (zero,) * (k + 1))
-        for other in range(k + 1):
-            fine_acc[k, other] = sums[other]
-
-        def aggregate(i, carry):
+        def last_planes(i, sums):
+            fine, rest = list(sums[: k + 1]), list(sums[k + 1 :])
+            found = {}
+            for plane in range(2):
+
+                def store(n, y, value, plane=plane):
+                    window = (2 * i + plane, slice(y, y + 8), slice((n - 1) * LANES, n * LANES))
+                    fields_ref[(k, *window)] = value
+                    for other in range(k):
+                        fine[other] = fine[other] + value * fields_ref[(other, *window)]
+                    fine[k] = fine[k] + value * value
+                    if plane:
+                        pairs[n - 1, y : y + 8, :] = found.pop((n, y)) + value
+                    else:
+                        found[n, y] = value
+
+                plane_sweep(s, k, 2 * i + 1 + plane, store)
+            halves = []
             for n in range(blocks):
-                columns = slice(n * LANES, (n + 1) * LANES)
-                for y in range(0, rows_y, 8):
-                    pairs[n, y : y + 8, :] = (
-                        fields_ref[k, 2 * i, y : y + 8, columns]
-                        + fields_ref[k, 2 * i + 1, y : y + 8, columns]
-                    )
-            for n in range(blocks):
-                columns = slice(n * LANES, (n + 1) * LANES)
-                quarter[i, :, columns] = (
+                value = (
                     pairs[n, pl.ds(0, half_y, stride=2), :]
                     + pairs[n, pl.ds(1, half_y, stride=2), :]
                 )
-            return carry
-
-        lax.fori_loop(0, half_x, aggregate, 0)
-        for n in range(0, blocks, 2):
-            whole = quarter[:, :, n * LANES : (n + 2) * LANES]
-            whole = whole.reshape(half_x * half_y, 2 * LANES)
-            total = None
-            for _ in range(3):
-                part = whole.astype(jnp.bfloat16)
-                whole = whole - part.astype(jnp.float32)
-                product = jnp.dot(part, pick, preferred_element_type=jnp.float32)
-                total = product if total is None else total + product
-            columns = slice(n // 2 * LANES, (n // 2 + 1) * LANES)
-            coarse_ref[k, :, :, columns] = total.reshape(half_x, half_y, LANES)
-
-        def coarse_products(i, sums):
-            sums = list(sums)
+                value = value + pltpu.roll(value, LANES - 1, 1)
+                halves.append(jnp.take_along_axis(value, compact, axis=1))
             for n in range(blocks // 2):
-                columns = slice(n * LANES, (n + 1) * LANES)
-                value = coarse_ref[k, i, :, columns]
+                value = 0.125 * jnp.where(lane < LANES // 2, halves[2 * n], halves[2 * n + 1])
+                window = (i, slice(None), slice(n * LANES, (n + 1) * LANES))
+                coarse_ref[(k, *window)] = value
                 for other in range(k):
-                    sums[other] = sums[other] + value * coarse_ref[other, i, :, columns]
-                sums[k] = sums[k] + value * value
-            return tuple(sums)
-
-        sums = lax.fori_loop(0, half_x, coarse_products, (zero,) * (k + 1))
+                    rest[other] = rest[other] + value * coarse_ref[(other, *window)]
+                rest[k] = rest[k] + value * value
+            return (*fine, *rest)
+
+        sums = lax.fori_loop(0, half_x, last_planes, (zero,) * (2 * k + 2))
         for other in range(k + 1):
-            coarse_acc[k, other] = sums[other]
+            fine_acc[k, other] = sums[other]
+            coarse_acc[k, other] = sums[k + 1 + other]
 
     part = zero
     for which, acc in enumerate((fine_acc, coarse_acc)):
@@ -459,11 +437,11 @@
         in_specs=[smem, hbm],
         out_specs=(vmem, vmem, vmem),
         scratch_shapes=[
-            pltpu.VMEM((2, vectors, rows_x + 2, (blocks + 2) * rows_y, LANES), f32),
+            pltpu.VMEM((vectors, rows_x + 2, (blocks + 2) * rows_y, LANES), f32),
+            pltpu.VMEM((vectors, rows_x + 2, (blocks + 2) * rows_y, LANES), f32),
             pltpu.VMEM((SWEEPS, 2, vectors, rows_x, blocks, LANES), f32),
             pltpu.VMEM((SWEEPS, 2, vectors, rows_x, blocks, LANES), f32),
             pltpu.VMEM((blocks, rows_y, LANES), f32),
-            pltpu.VMEM((rows_x // 2, rows_y // 2, rows_z), f32),
             pltpu.VMEM((vectors, vectors, 8, LANES), f32),
             pltpu.VMEM((vectors, vectors, 8, LANES), f32),
             pltpu.VMEM((sizes["gz"], 8, LANES), f32),

time: 98.5 us -> 76 us (0.77)
  Pallas kernels: 96.3 us -> 73.7 us
    pallas_call x1, Pallas kernels: 90.5 us -> 68 us  [local(): pl.pallas_call(functools.partial(sweep_kernel, sizes), out_shape=(pltpu.V...]
where the time goes in v2:
time: 76 us; the launch traced here: 75.1 us
  Pallas kernels  73.7 us (97%)
  local copies, waits for them, and re-layouts  0.77 us (1%)
    pallas_call x1, Pallas kernels, local(): pl.pallas_call(functools.partial(sweep_kernel, sizes), out_shape=(pltpu.V...  68 us
    pallas_call x1, Pallas kernels, local(): pl.pallas_call(functools.partial(basis_kernel, cells), out_shape=(jax.Sha...  5.75 us

profile of v2, /device:TPU:1, one launch (start us, length us, event | category | flops | bytes accessed | tf_op | source)
XLA Modules:
  0.0 75.1 jit_solution(3571460189967446717)
XLA Ops:
  0.6 0.8 %copy.4.aniso_ref = s32[3,2]{1,0:T(4,128)S(1)} copy(s32[3,2]{0,1:T(2,128)} %param.3) | data formatting | bytes 48 | tf_op args[1]
  1.4 68.0 %sweeps.1 = (f32[8,16,16,1024]{3,2,1,0:T(8,128)S(1)}, f32[8,8,8,512]{3,2,1,0:T(8,128)S(1)}, f32[8,128]{1,0:T(8,128)S(1)}) custom-call(s32[3,2]{1,0:T(4,128)S(1)} %copy.4.aniso_ref, f32[8,16,16,1024]{3,2,1,0:T(8,128)} %in_ref.1), custom_call_target="tpu_custom_call" | custom-call | tf_op jit(solution)/shard_map/sweeps/pallas_call | solution.py:430
  69.4 5.8 %basis.1 = (f32[8,16,16,1024]{3,2,1,0:T(8,128)}, f32[8,8,8,512]{3,2,1,0:T(8,128)}) custom-call(f32[8,128]{1,0:T(8,128)S(1)} %get-tuple-element.5.gram_ref, f32[8,16,16,1024]{3,2,1,0:T(8,128)S(1)} %get-tuple-element.6.fields_ref, f32[8,8,8,512]{3,2,1,0:T(8,128)S(1)} %get-tuple-element.7.coarse_ref), custom_call_target="tpu_custom_call" | custom-call | tf_op jit(solution)/shard_map/basis/pallas_call | solution.py:462

commit v3 on v2

--- a/solution.py
+++ b/solution.py
@@ -1,4 +1,5 @@
 import functools
+import itertools
 
 import jax
 import jax.numpy as jnp
@@ -13,30 +14,54 @@
 SWEEPS = 3
 LANES = 128
 AXES = ("gx", "gy", "gz")
+UNROLL = 8
+UNROLL_LAST = 4
+UNROLL_HALF = 2
+
+
+NEAR = ("gz",)
+FAR = ("gx", "gy")
+
+
+def others(sizes, axes):
+    return [o for o in itertools.product(*(range(sizes[a]) for a in axes)) if any(o)]
+
+
+def shifted(sizes, position, axes, offsets):
+    return {a: lax.rem(position[a] + o, sizes[a]) for a, o in zip(axes, offsets)}
+
+
+def slot_of(sizes, where, axes):
+    slot = 0
+    for axis in axes:
+        slot = slot * sizes[axis] + where[axis]
+    return slot
 
 
 def sweep_kernel(
     sizes,
-    aniso_ref,
+    aniso_hbm,
     in_ref,
     fields_ref,
     coarse_ref,
     gram_ref,
+    aniso_ref,
     even_state,
     odd_state,
     ysend,
     yrecv,
     pairs,
-    fine_acc,
-    coarse_acc,
-    gather_z,
-    gather_y,
-    gather_x,
+    sums_z,
+    gather_near,
+    gather_far,
+    aniso_sem,
     load_sem,
     send_sem,
     recv_sem,
-    gsend_sem,
-    grecv_sem,
+    near_send,
+    near_recv,
+    far_send,
+    far_recv,
 ):
     rows_x, rows_y, blocks = (in_ref.shape[1], in_ref.shape[2], in_ref.shape[3] // LANES)
     area = blocks * rows_y
@@ -55,15 +80,19 @@
             load(k, block).start()
         return carry
 
+    fetch = pltpu.make_async_copy(aniso_hbm, aniso_ref, aniso_sem)
+    fetch.start()
     lax.fori_loop(0, K, start_loads, 0)
 
     barrier = pltpu.get_barrier_semaphore()
     peers = 0
-    for axis in AXES:
-        for offset in range(1, sizes[axis]):
-            peer = lax.rem(position[axis] + offset, sizes[axis])
-            pl.semaphore_signal(barrier, inc=1, device_id={axis: peer}, device_id_type=MESH)
+    for axes in (NEAR, FAR):
+        for offsets in others(sizes, axes):
+            target = shifted(sizes, position, axes, offsets)
+            pl.semaphore_signal(barrier, inc=1, device_id=target, device_id_type=MESH)
             peers += 1
+
+    fetch.wait()
 
     def as_float(d, j):
         return jnp.full((8, LANES), aniso_ref[d, j], jnp.int32).astype(jnp.float32)
@@ -218,103 +247,125 @@
                 plane_sweep(s, k, x, store)
                 return carry
 
-            lax.fori_loop(1, rows_x + 1, one_plane, 0, unroll=4)
+            lax.fori_loop(1, rows_x + 1, one_plane, 0, unroll=UNROLL)
             send(s + 1, k)
             return carry
 
         lax.fori_loop(0, K, one_vector, 0)
 
     half_x, half_y = rows_x // 2, rows_y // 2
-    compact = lax.rem(2 * lane, LANES)
+    even = lax.rem(lane, 2) == 0
+    part = zero
     s = SWEEPS - 1
+
+    def add_products(part, k, first, sums):
+        stacked = zero
+        for other in range(k + 1):
+            summed = jnp.sum(sums[other], axis=0, keepdims=True)
+            stacked = jnp.where(row == other, summed, stacked)
+        column = jnp.broadcast_to(jnp.sum(stacked, axis=1, keepdims=True), (8, LANES))
+        across = jnp.sum(jnp.where(lane == row + first, column, 0.0), axis=0, keepdims=True)
+        part = jnp.where((lane == first + k) & (row <= k), column, part)
+        inside = (row == k) & (lane >= first) & (lane < first + k)
+        return jnp.where(inside, jnp.broadcast_to(across, (8, LANES)), part)
+
     for k in range(K):
         wait_faces(s, k)
 
-        def last_planes(i, sums):
-            fine, rest = list(sums[: k + 1]), list(sums[k + 1 :])
-            found = {}
-            for plane in range(2):
-
-                def store(n, y, value, plane=plane):
-                    window = (2 * i + plane, slice(y, y + 8), slice((n - 1) * LANES, n * LANES))
-                    fields_ref[(k, *window)] = value
-                    for other in range(k):
-                        fine[other] = fine[other] + value * fields_ref[(other, *window)]
-                    fine[k] = fine[k] + value * value
-                    if plane:
-                        pairs[n - 1, y : y + 8, :] = found.pop((n, y)) + value
-                    else:
-                        found[n, y] = value
-
-                plane_sweep(s, k, 2 * i + 1 + plane, store)
-            halves = []
+        def last_plane(x, sums):
+            fine = list(sums)
+
+            def store(n, y, value):
+                window = (x - 1, slice(y, y + 8), slice((n - 1) * LANES, n * LANES))
+                fields_ref[(k, *window)] = value
+                for other in range(k):
+                    fine[other] = fine[other] + value * fields_ref[(other, *window)]
+                fine[k] = fine[k] + value * value
+
+            plane_sweep(s, k, x, store)
+            return tuple(fine)
+
+        fine = lax.fori_loop(1, rows_x + 1, last_plane, (zero,) * (k + 1), unroll=UNROLL_LAST)
+
+        def aggregate(i, sums):
+            rest = list(sums)
+            for n in range(blocks):
+                columns = slice(n * LANES, (n + 1) * LANES)
+                for y in range(0, rows_y, 8):
+                    pairs[n, y : y + 8, :] = (
+                        fields_ref[k, 2 * i, y : y + 8, columns]
+                        + fields_ref[k, 2 * i + 1, y : y + 8, columns]
+                    )
             for n in range(blocks):
                 value = (
                     pairs[n, pl.ds(0, half_y, stride=2), :]
                     + pairs[n, pl.ds(1, half_y, stride=2), :]
                 )
-                value = value + pltpu.roll(value, LANES - 1, 1)
-                halves.append(jnp.take_along_axis(value, compact, axis=1))
-            for n in range(blocks // 2):
-                value = 0.125 * jnp.where(lane < LANES // 2, halves[2 * n], halves[2 * n + 1])
-                window = (i, slice(None), slice(n * LANES, (n + 1) * LANES))
-                coarse_ref[(k, *window)] = value
+                value = 0.125 * (value + pltpu.roll(value, LANES - 1, 1))
+                value = jnp.where(even, value, 0.0)
+                sums_z[k, i, n] = value
                 for other in range(k):
-                    rest[other] = rest[other] + value * coarse_ref[(other, *window)]
+                    rest[other] = rest[other] + value * sums_z[other, i, n]
                 rest[k] = rest[k] + value * value
-            return (*fine, *rest)
-
-        sums = lax.fori_loop(0, half_x, last_planes, (zero,) * (2 * k + 2))
-        for other in range(k + 1):
-            fine_acc[k, other] = sums[other]
-            coarse_acc[k, other] = sums[k + 1 + other]
-
-    part = zero
-    for which, acc in enumerate((fine_acc, coarse_acc)):
-        for k in range(K):
-            stacked = zero
-            for other in range(K):
-                tile = acc[max(k, other), min(k, other)]
-                summed = jnp.sum(tile, axis=0, keepdims=True)
-                stacked = jnp.where(row == other, summed, stacked)
-            column = jnp.sum(stacked, axis=1, keepdims=True)
-            part = jnp.where(lane == which * K + k, column, part)
-
-    for number, (axis, slots) in enumerate((("gz", gather_z), ("gy", gather_y), ("gx", gather_x))):
-        count = sizes[axis]
-        me = position[axis]
+            return tuple(rest)
+
+        rest = lax.fori_loop(0, half_x, aggregate, (zero,) * (k + 1), unroll=UNROLL_HALF)
+        part = add_products(part, k, 0, fine)
+        part = add_products(part, k, K, rest)
+
+    def pack_lanes(k, carry):
+        index = lax.rem(2 * lane, LANES)
+        for i in range(half_x):
+            for n in range(0, blocks, 2):
+                low = jnp.take_along_axis(sums_z[k, i, n], index, axis=1)
+                high = jnp.take_along_axis(sums_z[k, i, n + 1], index, axis=1)
+                window = (i, slice(None), slice(n // 2 * LANES, (n // 2 + 1) * LANES))
+                coarse_ref[(k, *window)] = jnp.where(lane < LANES // 2, low, high)
+        return carry
+
+    stages = (
+        (NEAR, gather_near, near_send, near_recv),
+        (FAR, gather_far, far_send, far_recv),
+    )
+    for stage, (axes, slots, sent, received) in enumerate(stages):
+        me = slot_of(sizes, position, axes)
+        group = others(sizes, axes)
         slots[me] = part
 
-        def exchange(offset, axis=axis, slots=slots, me=me, count=count, number=number):
+        def exchange(number, axes=axes, slots=slots, me=me, group=group, sent=sent, received=received):
             return pltpu.make_async_remote_copy(
                 src_ref=slots.at[me],
                 dst_ref=slots.at[me],
-                send_sem=gsend_sem.at[number, offset],
-                recv_sem=grecv_sem.at[number, offset],
-                device_id={axis: lax.rem(me + offset, count)},
+                send_sem=sent.at[number],
+                recv_sem=received.at[number],
+                device_id=shifted(sizes, position, axes, group[number]),
                 device_id_type=MESH,
             )
 
-        def arrival(offset, axis=axis, slots=slots, me=me, count=count, number=number):
-            source = lax.rem(me + count - offset, count)
+        def arrival(number, axes=axes, slots=slots, group=group, sent=sent, received=received):
+            back = tuple(sizes[a] - o for a, o in zip(axes, group[number]))
+            where = shifted(sizes, position, axes, back)
+            source = slot_of(sizes, where, axes)
             return pltpu.make_async_remote_copy(
                 src_ref=slots.at[source],
                 dst_ref=slots.at[source],
-                send_sem=gsend_sem.at[number, offset],
-                recv_sem=grecv_sem.at[number, offset],
-                device_id={axis: source},
+                send_sem=sent.at[number],
+                recv_sem=received.at[number],
+                device_id=where,
                 device_id_type=MESH,
             )
 
-        for offset in range(1, count):
-            exchange(offset).start()
-        for offset in range(1, count):
-            arrival(offset).wait_recv()
+        for number in range(len(group)):
+            exchange(number).start()
+        half = K // 2
+        lax.fori_loop(stage * half, (stage + 1) * half, pack_lanes, 0)
+        for number in range(len(group)):
+            arrival(number).wait_recv()
         part = slots[0]
-        for slot in range(1, count):
+        for slot in range(1, len(group) + 1):
             part = part + slots[slot]
-        for offset in range(1, count):
-            exchange(offset).wait_send()
+        for number in range(len(group)):
+            exchange(number).wait_send()
     gram_ref[...] = part
 
     def finish(k, carry):
@@ -424,9 +475,8 @@
     half = (vectors, rows_x // 2, rows_y // 2, rows_z // 2)
     f32 = jnp.float32
     hbm = pl.BlockSpec(memory_space=pltpu.HBM)
-    smem = pl.BlockSpec(memory_space=pltpu.SMEM)
     vmem = pl.BlockSpec(memory_space=pltpu.VMEM)
-    longest = max(sizes.values())
+    near, far = len(others(sizes, NEAR)), len(others(sizes, FAR))
     fields, coarse, gram = pl.pallas_call(
         functools.partial(sweep_kernel, sizes),
         out_shape=(
@@ -434,24 +484,26 @@
             pltpu.VMEM(half, f32),
             pltpu.VMEM((8, LANES), f32),
         ),
-        in_specs=[smem, hbm],
+        in_specs=[hbm, hbm],
         out_specs=(vmem, vmem, vmem),
         scratch_shapes=[
+            pltpu.SMEM(aniso.shape, jnp.int32),
             pltpu.VMEM((vectors, rows_x + 2, (blocks + 2) * rows_y, LANES), f32),
             pltpu.VMEM((vectors, rows_x + 2, (blocks + 2) * rows_y, LANES), f32),
             pltpu.VMEM((SWEEPS, 2, vectors, rows_x, blocks, LANES), f32),
             pltpu.VMEM((SWEEPS, 2, vectors, rows_x, blocks, LANES), f32),
             pltpu.VMEM((blocks, rows_y, LANES), f32),
-            pltpu.VMEM((vectors, vectors, 8, LANES), f32),
-            pltpu.VMEM((vectors, vectors, 8, LANES), f32),
-            pltpu.VMEM((sizes["gz"], 8, LANES), f32),
-            pltpu.VMEM((sizes["gy"], 8, LANES), f32),
-            pltpu.VMEM((sizes["gx"], 8, LANES), f32),
+            pltpu.VMEM((vectors, rows_x // 2, blocks, rows_y // 2, LANES), f32),
+            pltpu.VMEM((near + 1, 8, LANES), f32),
+            pltpu.VMEM((far + 1, 8, LANES), f32),
+            pltpu.SemaphoreType.DMA(()),
             pltpu.SemaphoreType.DMA((vectors, blocks)),
             pltpu.SemaphoreType.DMA((6, SWEEPS, vectors)),
             pltpu.SemaphoreType.DMA((6, SWEEPS, vectors)),
-            pltpu.SemaphoreType.DMA((3, longest)),
-            pltpu.SemaphoreType.DMA((3, longest)),
+            pltpu.SemaphoreType.DMA((near,)),
+            pltpu.SemaphoreType.DMA((near,)),
+            pltpu.SemaphoreType.DMA((far,)),
+            pltpu.SemaphoreType.DMA((far,)),
         ],
         compiler_params=pltpu.CompilerParams(
             collective_id=0, has_side_effects=True, vmem_limit_bytes=44 * 1024 * 1024

time: 76 us -> 66.9 us (0.88); the launches traced: 75.1 us -> 66.8 us
  Pallas kernels: 73.7 us -> 65.4 us
    pallas_call x1, Pallas kernels: 68 us -> 59.6 us  [local(): pl.pallas_call(functools.partial(sweep_kernel, sizes), out_shape=(pltpu.V...]
where the time goes in v3:
time: 66.9 us; the launch traced here: 66.8 us
  Pallas kernels  65.4 us (98%)
  local copies, waits for them, and re-layouts  0.77 us (1%)
    pallas_call x1, Pallas kernels, local(): pl.pallas_call(functools.partial(sweep_kernel, sizes), out_shape=(pltpu.V...  59.6 us
    pallas_call x1, Pallas kernels, local(): pl.pallas_call(functools.partial(basis_kernel, cells), out_shape=(jax.Sha...  5.75 us

profile of v3, /device:TPU:1, one launch (start us, length us, event | category | flops | bytes accessed | tf_op | source)
XLA Modules:
  0.0 66.8 jit_solution(1796377510819983598)
XLA Ops:
  0.6 0.8 %copy.4.aniso_hbm = s32[3,2]{1,0:T(4,128)S(1)} copy(s32[3,2]{0,1:T(2,128)} %param.3) | data formatting | bytes 48 | tf_op args[1]
  1.4 59.6 %sweeps.1 = (f32[8,16,16,1024]{3,2,1,0:T(8,128)S(1)}, f32[8,8,8,512]{3,2,1,0:T(8,128)S(1)}, f32[8,128]{1,0:T(8,128)S(1)}) custom-call(s32[3,2]{1,0:T(4,128)S(1)} %copy.4.aniso_hbm, f32[8,16,16,1024]{3,2,1,0:T(8,128)} %in_ref.1), custom_call_target="tpu_custom_call" | custom-call | tf_op jit(solution)/shard_map/sweeps/pallas_call | solution.py:480
  61.0 5.8 %basis.1 = (f32[8,16,16,1024]{3,2,1,0:T(8,128)}, f32[8,8,8,512]{3,2,1,0:T(8,128)}) custom-call(f32[8,128]{1,0:T(8,128)S(1)} %get-tuple-element.5.gram_ref, f32[8,16,16,1024]{3,2,1,0:T(8,128)S(1)} %get-tuple-element.6.fields_ref, f32[8,8,8,512]{3,2,1,0:T(8,128)S(1)} %get-tuple-element.7.coarse_ref), custom_call_target="tpu_custom_call" | custom-call | tf_op jit(solution)/shard_map/basis/pallas_call | solution.py:514

commit v4 on v3

--- a/solution.py
+++ b/solution.py
@@ -15,8 +15,9 @@
 LANES = 128
 AXES = ("gx", "gy", "gz")
 UNROLL = 8
-UNROLL_LAST = 4
-UNROLL_HALF = 2
+GROUPS = (1,) * 8
+UNROLL_LAST = 8
+UNROLL_HALF = 4
 
 
 NEAR = ("gz",)
@@ -92,39 +93,32 @@
             pl.semaphore_signal(barrier, inc=1, device_id=target, device_id_type=MESH)
             peers += 1
 
-    fetch.wait()
-
-    def as_float(d, j):
-        return jnp.full((8, LANES), aniso_ref[d, j], jnp.int32).astype(jnp.float32)
-
-    coefficients = [as_float(d, 0) / as_float(d, 1) for d in range(3)]
-    scaled = omega_weight / (2.0 * (coefficients[0] + coefficients[1] + coefficients[2]))
-    weights = [scaled * c for c in coefficients]
-    keep = 1.0 - omega_weight
-
     lane = lax.broadcasted_iota(jnp.int32, (8, LANES), 1)
     row = lax.broadcasted_iota(jnp.int32, (8, LANES), 0)
 
-    def face(s, k, direction):
+    starts = [sum(GROUPS[:g]) for g in range(len(GROUPS))]
+
+    def face(s, g, direction):
+        vectors = pl.ds(starts[g], GROUPS[g])
         state = states[s % 2]
         axis, side = AXES[direction // 2], direction % 2
         peer = position[axis] + (1 if side else -1)
         if axis == "gx":
-            source = state.at[k, rows_x if side else 1, pl.ds(rows_y, area), :]
-            target = state.at[k, 0 if side else rows_x + 1, pl.ds(rows_y, area), :]
+            source = state.at[vectors, rows_x if side else 1, pl.ds(rows_y, area), :]
+            target = state.at[vectors, 0 if side else rows_x + 1, pl.ds(rows_y, area), :]
         elif axis == "gy":
-            source = ysend.at[s, side, k]
-            target = yrecv.at[s, side, k]
+            source = ysend.at[s, side, vectors]
+            target = yrecv.at[s, side, vectors]
         else:
             from_row = blocks * rows_y if side else rows_y
             to_row = 0 if side else (blocks + 1) * rows_y
-            source = state.at[k, pl.ds(1, rows_x), pl.ds(from_row, rows_y), :]
-            target = state.at[k, pl.ds(1, rows_x), pl.ds(to_row, rows_y), :]
+            source = state.at[vectors, pl.ds(1, rows_x), pl.ds(from_row, rows_y), :]
+            target = state.at[vectors, pl.ds(1, rows_x), pl.ds(to_row, rows_y), :]
         return pltpu.make_async_remote_copy(
             src_ref=source,
             dst_ref=target,
-            send_sem=send_sem.at[direction, s, k],
-            recv_sem=recv_sem.at[direction, s, k],
+            send_sem=send_sem.at[direction, s, g],
+            recv_sem=recv_sem.at[direction, s, g],
             device_id={axis: peer},
             device_id_type=MESH,
         )
@@ -136,35 +130,37 @@
     def can_receive(direction):
         return can_send(direction ^ 1)
 
-    def send(s, k):
+    def pack(s, k):
         state = states[s % 2]
 
-        def pack(x, carry):
+        def pack_plane(x, carry):
             for side in range(2):
                 first = rows_y + (rows_y - 1 if side else 0)
                 ysend[s, side, k, x] = state[k, x + 1, pl.ds(first, blocks, stride=rows_y), :]
             return carry
 
-        lax.fori_loop(0, rows_x, pack, 0, unroll=4)
+        lax.fori_loop(0, rows_x, pack_plane, 0, unroll=4)
+
+    def send(s, g):
         for direction in range(6):
 
             @pl.when(can_send(direction))
             def _():
-                face(s, k, direction).start()
-
-    def wait_faces(s, k):
+                face(s, g, direction).start()
+
+    def wait_faces(s, g):
         for direction in range(6):
 
             @pl.when(can_receive(direction))
             def _():
-                face(s, k, direction).wait_recv()
-
-    def wait_sent(s, k):
+                face(s, g, direction).wait_recv()
+
+    def wait_sent(s, g):
         for direction in range(6):
 
             @pl.when(can_send(direction))
             def _():
-                face(s, k, direction).wait_send()
+                face(s, g, direction).wait_send()
 
     zero = jnp.zeros((8, LANES), jnp.float32)
 
@@ -191,21 +187,33 @@
 
         lax.fori_loop(0, K, clear_one, 0)
 
+    pl.semaphore_wait(barrier, peers)
+
+    def loaded(k, carry):
+        for block in range(blocks):
+            load(k, block).wait()
+        pack(0, k)
+        return carry
+
+    for g, size in enumerate(GROUPS):
+        lax.fori_loop(starts[g], starts[g] + size, loaded, 0)
+        send(0, g)
+
     for direction in range(6):
 
         @pl.when(jnp.logical_not(can_receive(direction)))
         def _():
             clear(direction)
 
-    pl.semaphore_wait(barrier, peers)
-
-    def first_sends(k, carry):
-        for block in range(blocks):
-            load(k, block).wait()
-        send(0, k)
-        return carry
-
-    lax.fori_loop(0, K, first_sends, 0)
+    fetch.wait()
+
+    def as_float(d, j):
+        return jnp.full((8, LANES), aniso_ref[d, j], jnp.int32).astype(jnp.float32)
+
+    coefficients = [as_float(d, 0) / as_float(d, 1) for d in range(3)]
+    scaled = omega_weight / (2.0 * (coefficients[0] + coefficients[1] + coefficients[2]))
+    weights = [scaled * c for c in coefficients]
+    keep = 1.0 - omega_weight
 
     def plane_sweep(s, k, x, store):
         state = states[s % 2]
@@ -232,26 +240,27 @@
                 store(n, y, value)
 
     for s in range(SWEEPS - 1):
-
-        def one_vector(k, carry, s=s):
-            wait_faces(s, k)
+        for g, size in enumerate(GROUPS):
+            wait_faces(s, g)
             if s > 0:
-                wait_sent(s - 1, k)
+                wait_sent(s - 1, g)
             after = states[(s + 1) % 2]
 
-            def one_plane(x, carry):
-                def store(n, y, value):
-                    r = n * rows_y + y
-                    after[k, x, r : r + 8, :] = value
-
-                plane_sweep(s, k, x, store)
+            def one_vector(k, carry, s=s, after=after):
+                def one_plane(x, carry):
+                    def store(n, y, value):
+                        r = n * rows_y + y
+                        after[k, x, r : r + 8, :] = value
+
+                    plane_sweep(s, k, x, store)
+                    return carry
+
+                lax.fori_loop(1, rows_x + 1, one_plane, 0, unroll=UNROLL)
+                pack(s + 1, k)
                 return carry
 
-            lax.fori_loop(1, rows_x + 1, one_plane, 0, unroll=UNROLL)
-            send(s + 1, k)
-            return carry
-
-        lax.fori_loop(0, K, one_vector, 0)
+            lax.fori_loop(starts[g], starts[g] + size, one_vector, 0)
+            send(s + 1, g)
 
     half_x, half_y = rows_x // 2, rows_y // 2
     even = lax.rem(lane, 2) == 0
@@ -270,7 +279,8 @@
         return jnp.where(inside, jnp.broadcast_to(across, (8, LANES)), part)
 
     for k in range(K):
-        wait_faces(s, k)
+        if k in starts:
+            wait_faces(s, starts.index(k))
 
         def last_plane(x, sums):
             fine = list(sums)
@@ -286,6 +296,8 @@
             return tuple(fine)
 
         fine = lax.fori_loop(1, rows_x + 1, last_plane, (zero,) * (k + 1), unroll=UNROLL_LAST)
+
+        part = add_products(part, k, 0, fine)
 
         def aggregate(i, sums):
             rest = list(sums)
@@ -310,7 +322,6 @@
             return tuple(rest)
 
         rest = lax.fori_loop(0, half_x, aggregate, (zero,) * (k + 1), unroll=UNROLL_HALF)
-        part = add_products(part, k, 0, fine)
         part = add_products(part, k, K, rest)
 
     def pack_lanes(k, carry):
@@ -368,25 +379,31 @@
             exchange(number).wait_send()
     gram_ref[...] = part
 
-    def finish(k, carry):
-        for s in range(SWEEPS - 2, SWEEPS):
-            wait_sent(s, k)
-        return carry
-
-    lax.fori_loop(0, K, finish, 0)
-
-
-def inverse_factor(gram, lane, row):
-    work = jnp.where(lane < K, gram, 0.0) + jnp.where(lane == row + K, 1.0, 0.0)
+    for s in range(SWEEPS - 2, SWEEPS):
+        for g in range(len(GROUPS)):
+            wait_sent(s, g)
+
+
+def inverse_factor(entry):
+    left = {(k, j): entry(k, j) for k in range(K) for j in range(k + 1)}
+    factor, inverse, scale = {}, {}, []
     for j in range(K):
-        pivot_row = jnp.broadcast_to(work[j : j + 1, :], work.shape)
-        column = jnp.broadcast_to(work[:, j : j + 1], work.shape)
-        pivot = jnp.broadcast_to(pivot_row[:, j : j + 1], work.shape)
-        factor = jnp.where(row > j, column / pivot, 0.0)
-        work = work - factor * pivot_row
-    pivots = jnp.sum(jnp.where(lane == row, work, 0.0), axis=1, keepdims=True)
-    scale = 1.0 / jnp.sqrt(pivots)
-    return pltpu.roll(work * scale, LANES - K, 1)
+        scale.append(lax.rsqrt(left[j, j]))
+        reciprocal = 1.0 / left[j, j]
+        for k in range(j + 1, K):
+            factor[k, j] = left[k, j] * reciprocal
+        for k in range(j + 1, K):
+            for other in range(j + 1, k + 1):
+                left[k, other] = left[k, other] - factor[k, j] * left[other, j]
+    for k in range(K):
+        for j in range(k):
+            total = factor[k, j]
+            for other in range(j + 1, k):
+                total = total + factor[k, other] * inverse[other, j]
+            inverse[k, j] = -total
+    result = {(k, j): scale[k] * inverse[k, j] for k in range(K) for j in range(k)}
+    result.update({(k, k): scale[k] for k in range(K)})
+    return result
 
 
 def basis_kernel(
@@ -398,6 +415,7 @@
     coarse_basis_ref,
     stage,
     coarse_stage,
+    columns,
     table,
     out_sem,
     coarse_sem,
@@ -407,21 +425,26 @@
         fields_ref.shape[2],
         fields_ref.shape[3] // LANES,
     )
-    lane = lax.broadcasted_iota(jnp.int32, (8, LANES), 1)
-    row = lax.broadcasted_iota(jnp.int32, (8, LANES), 0)
     gram = gram_ref[...]
-    fine = inverse_factor(gram / cells, lane, row)
-    rest = inverse_factor(pltpu.roll(gram, LANES - K, 1) / (cells // 8), lane, row)
-    for which, inverse in enumerate((fine, rest)):
-        for other in range(K):
-            table[which, other] = jnp.broadcast_to(inverse[:, other : other + 1], (8, LANES))
+    for which, count in enumerate((cells, cells // 8)):
+        mean = gram / count
+        for j in range(K):
+            c = which * K + j
+            columns[c] = jnp.broadcast_to(mean[:, c : c + 1], (8, LANES))
+    for which in range(2):
+
+        def entry(k, j, which=which):
+            return jnp.broadcast_to(columns[which * K + j, k : k + 1, :], (8, LANES))
+
+        for (k, j), value in inverse_factor(entry).items():
+            table[which, k * (k + 1) // 2 + j] = value
 
     def combine(which, windows, source, target):
         loaded = [[source(other, w) for w in windows] for other in range(K)]
         for k in range(K):
             totals = None
             for other in range(k + 1):
-                weight = jnp.broadcast_to(table[which, other, k : k + 1, :], (8, LANES))
+                weight = table[which, k * (k + 1) // 2 + other]
                 products = [weight * value for value in loaded[other]]
                 totals = (
                     products if totals is None else [t + p for t, p in zip(totals, products)]
@@ -445,8 +468,6 @@
         put(x).start()
         return carry
 
-    lax.fori_loop(0, rows_x, one_plane, 0)
-
     def one_coarse(x, carry):
         def source(k, n):
             return coarse_ref[k, x, :, n * LANES : (n + 1) * LANES]
@@ -457,9 +478,11 @@
         combine(1, list(range(blocks // 2)), source, target)
         return carry
 
+    lax.fori_loop(0, rows_x // 2, one_plane, 0)
     lax.fori_loop(0, rows_x // 2, one_coarse, 0)
     out = pltpu.make_async_copy(coarse_stage, coarse_basis_ref, coarse_sem)
     out.start()
+    lax.fori_loop(rows_x // 2, rows_x, one_plane, 0)
 
     def drain(x, carry):
         put(x).wait()
@@ -498,8 +521,8 @@
             pltpu.VMEM((far + 1, 8, LANES), f32),
             pltpu.SemaphoreType.DMA(()),
             pltpu.SemaphoreType.DMA((vectors, blocks)),
-            pltpu.SemaphoreType.DMA((6, SWEEPS, vectors)),
-            pltpu.SemaphoreType.DMA((6, SWEEPS, vectors)),
+            pltpu.SemaphoreType.DMA((6, SWEEPS, len(GROUPS))),
+            pltpu.SemaphoreType.DMA((6, SWEEPS, len(GROUPS))),
             pltpu.SemaphoreType.DMA((near,)),
             pltpu.SemaphoreType.DMA((near,)),
             pltpu.SemaphoreType.DMA((far,)),
@@ -522,7 +545,8 @@
         scratch_shapes=[
             pltpu.VMEM((rows_x, vectors, rows_y, rows_z), f32),
             pltpu.VMEM(half, f32),
-            pltpu.VMEM((2, vectors, 8, LANES), f32),
+            pltpu.VMEM((2 * vectors, 8, LANES), f32),
+            pltpu.VMEM((2, vectors * (vectors + 1) // 2, 8, LANES), f32),
             pltpu.SemaphoreType.DMA((rows_x,)),
             pltpu.SemaphoreType.DMA(()),
         ],

time: 66.9 us -> 64.6 us (0.966)
  Pallas kernels: 65.4 us -> 63 us
    pallas_call x1, Pallas kernels: 5.75 us -> 4.26 us  [local(): pl.pallas_call(functools.partial(basis_kernel, cells), out_shape=(jax.Sha...]
    pallas_call x1, Pallas kernels: 59.6 us -> 58.8 us  [local(): pl.pallas_call(functools.partial(sweep_kernel, sizes), out_shape=(pltpu.V...]
where the time goes in v4:
time: 64.6 us; the launch traced here: 64.5 us
  Pallas kernels  63 us (98%)
  local copies, waits for them, and re-layouts  0.77 us (1%)
    pallas_call x1, Pallas kernels, local(): pl.pallas_call(functools.partial(sweep_kernel, sizes), out_shape=(pltpu.V...  58.8 us
    pallas_call x1, Pallas kernels, local(): pl.pallas_call(functools.partial(basis_kernel, cells), out_shape=(jax.Sha...  4.26 us

profile of v4, /device:TPU:1, one launch (start us, length us, event | category | flops | bytes accessed | tf_op | source)
XLA Modules:
  0.0 64.5 jit_solution(17558889625225032928)
XLA Ops:
  0.6 0.8 %copy.4.aniso_hbm = s32[3,2]{1,0:T(4,128)S(1)} copy(s32[3,2]{0,1:T(2,128)} %param.3) | data formatting | bytes 48 | tf_op args[1]
  1.4 58.8 %sweeps.1 = (f32[8,16,16,1024]{3,2,1,0:T(8,128)S(1)}, f32[8,8,8,512]{3,2,1,0:T(8,128)S(1)}, f32[8,128]{1,0:T(8,128)S(1)}) custom-call(s32[3,2]{1,0:T(4,128)S(1)} %copy.4.aniso_hbm, f32[8,16,16,1024]{3,2,1,0:T(8,128)} %in_ref.1), custom_call_target="tpu_custom_call" | custom-call | tf_op jit(solution)/shard_map/sweeps/pallas_call | solution.py:503
  60.2 4.3 %basis.1 = (f32[8,16,16,1024]{3,2,1,0:T(8,128)}, f32[8,8,8,512]{3,2,1,0:T(8,128)}) custom-call(f32[8,128]{1,0:T(8,128)S(1)} %get-tuple-element.5.gram_ref, f32[8,16,16,1024]{3,2,1,0:T(8,128)S(1)} %get-tuple-element.6.fields_ref, f32[8,8,8,512]{3,2,1,0:T(8,128)S(1)} %get-tuple-element.7.coarse_ref), custom_call_target="tpu_custom_call" | custom-call | tf_op jit(solution)/shard_map/basis/pallas_call | solution.py:537

commit v5 on v4

--- a/solution.py
+++ b/solution.py
@@ -22,6 +22,13 @@
 
 NEAR = ("gz",)
 FAR = ("gx", "gy")
+ROUNDS = (
+    (("gz", 1), ("gx", 1)),
+    (("gz", 2), ("gx", 2)),
+    (("gz", 4), ("gy", 1)),
+    (("gy", 1),),
+    (("gy", 2),),
+)
 
 
 def others(sizes, axes):
@@ -63,6 +70,7 @@
     near_recv,
     far_send,
     far_recv,
+    rounds,
 ):
     rows_x, rows_y, blocks = (in_ref.shape[1], in_ref.shape[2], in_ref.shape[3] // LANES)
     area = blocks * rows_y
@@ -85,13 +93,29 @@
     fetch.start()
     lax.fori_loop(0, K, start_loads, 0)
 
+    def greet(semaphore, axis, distance):
+        heard = 0
+        for step in (-distance, distance):
+            there = position[axis] >= distance if step < 0 else position[axis] < sizes[axis] - distance
+
+            @pl.when(there)
+            def _():
+                pl.semaphore_signal(
+                    semaphore,
+                    inc=1,
+                    device_id={axis: position[axis] + step},
+                    device_id_type=MESH,
+                )
+
+            heard = heard + there.astype(jnp.int32)
+        return heard
+
     barrier = pltpu.get_barrier_semaphore()
-    peers = 0
-    for axes in (NEAR, FAR):
-        for offsets in others(sizes, axes):
-            target = shifted(sizes, position, axes, offsets)
-            pl.semaphore_signal(barrier, inc=1, device_id=target, device_id_type=MESH)
-            peers += 1
+    peers = sum(greet(barrier, axis, 1) for axis in AXES)
+
+    def hear(number):
+        heard = sum(greet(rounds.at[number], axis, d) for axis, d in ROUNDS[number])
+        pl.semaphore_wait(rounds.at[number], heard)
 
     lane = lax.broadcasted_iota(jnp.int32, (8, LANES), 1)
     row = lax.broadcasted_iota(jnp.int32, (8, LANES), 0)
@@ -208,7 +232,7 @@
     fetch.wait()
 
     def as_float(d, j):
-        return jnp.full((8, LANES), aniso_ref[d, j], jnp.int32).astype(jnp.float32)
+        return jnp.full((8, LANES), aniso_ref[j, d], jnp.int32).astype(jnp.float32)
 
     coefficients = [as_float(d, 0) / as_float(d, 1) for d in range(3)]
     scaled = omega_weight / (2.0 * (coefficients[0] + coefficients[1] + coefficients[2]))
@@ -261,6 +285,8 @@
 
             lax.fori_loop(starts[g], starts[g] + size, one_vector, 0)
             send(s + 1, g)
+            if s == 0 and 2 <= g < 2 + len(ROUNDS):
+                hear(g - 2)
 
     half_x, half_y = rows_x // 2, rows_y // 2
     even = lax.rem(lane, 2) == 0
@@ -510,7 +536,7 @@
         in_specs=[hbm, hbm],
         out_specs=(vmem, vmem, vmem),
         scratch_shapes=[
-            pltpu.SMEM(aniso.shape, jnp.int32),
+            pltpu.SMEM(aniso.shape[::-1], jnp.int32),
             pltpu.VMEM((vectors, rows_x + 2, (blocks + 2) * rows_y, LANES), f32),
             pltpu.VMEM((vectors, rows_x + 2, (blocks + 2) * rows_y, LANES), f32),
             pltpu.VMEM((SWEEPS, 2, vectors, rows_x, blocks, LANES), f32),
@@ -527,12 +553,13 @@
             pltpu.SemaphoreType.DMA((near,)),
             pltpu.SemaphoreType.DMA((far,)),
             pltpu.SemaphoreType.DMA((far,)),
+            pltpu.SemaphoreType.REGULAR((len(ROUNDS),)),
         ],
         compiler_params=pltpu.CompilerParams(
             collective_id=0, has_side_effects=True, vmem_limit_bytes=44 * 1024 * 1024
         ),
         name="sweeps",
-    )(aniso, test_vectors)
+    )(pltpu.with_memory_space_constraint(aniso.T, pltpu.HBM), test_vectors)
     cells = float(rows_x * rows_y * rows_z * sizes["gx"] * sizes["gy"] * sizes["gz"])
     return pl.pallas_call(
         functools.partial(basis_kernel, cells),

time: 64.6 us -> 62.5 us (0.967)
  Pallas kernels: 63 us -> 61.6 us
  local copies, waits for them, and re-layouts: 0.77 us -> 0 us
    pallas_call x1, Pallas kernels: 58.8 us -> 57.4 us  [local(): pl.pallas_call(functools.partial(sweep_kernel, sizes), out_shape=(pltpu.V...]
    unnamed x1 -> x0, local copies, waits for them, and re-layouts: 0.77 us -> none
where the time goes in v5:
time: 62.5 us; the launch traced here: 62.4 us
  Pallas kernels  61.6 us (99%)
  between operations  0.8 us (1%)
    pallas_call x1, Pallas kernels, local(): pl.pallas_call(functools.partial(sweep_kernel, sizes), out_shape=(pltpu.V...  57.4 us
    pallas_call x1, Pallas kernels, local(): pl.pallas_call(functools.partial(basis_kernel, cells), out_shape=(jax.Sha...  4.18 us

profile of v5, /device:TPU:1, one launch (start us, length us, event | category | flops | bytes accessed | tf_op | source)
XLA Modules:
  0.0 62.4 jit_solution(2883977167043156340)
XLA Ops:
  0.6 57.4 %sweeps.1 = (f32[8,16,16,1024]{3,2,1,0:T(8,128)S(1)}, f32[8,8,8,512]{3,2,1,0:T(8,128)S(1)}, f32[8,128]{1,0:T(8,128)S(1)}) custom-call(s32[2,3]{1,0:T(2,128)} %bitcast.1, f32[8,16,16,1024]{3,2,1,0:T(8,128)} %in_ref.1), custom_call_target="tpu_custom_call" | custom-call | tf_op jit(solution)/shard_map/sweeps/pallas_call | solution.py:529
  58.1 4.2 %basis.1 = (f32[8,16,16,1024]{3,2,1,0:T(8,128)}, f32[8,8,8,512]{3,2,1,0:T(8,128)}) custom-call(f32[8,128]{1,0:T(8,128)S(1)} %get-tuple-element.5.gram_ref, f32[8,16,16,1024]{3,2,1,0:T(8,128)S(1)} %get-tuple-element.6.fields_ref, f32[8,8,8,512]{3,2,1,0:T(8,128)S(1)} %get-tuple-element.7.coarse_ref), custom_call_target="tpu_custom_call" | custom-call | tf_op jit(solution)/shard_map/basis/pallas_call | solution.py:564

commit v6 on v5

--- a/solution.py
+++ b/solution.py
@@ -396,6 +396,8 @@
             exchange(number).start()
         half = K // 2
         lax.fori_loop(stage * half, (stage + 1) * half, pack_lanes, 0)
+        for g in range(len(GROUPS)):
+            wait_sent(SWEEPS - 2 + stage, g)
         for number in range(len(group)):
             arrival(number).wait_recv()
         part = slots[0]
@@ -404,10 +406,6 @@
         for number in range(len(group)):
             exchange(number).wait_send()
     gram_ref[...] = part
-
-    for s in range(SWEEPS - 2, SWEEPS):
-        for g in range(len(GROUPS)):
-            wait_sent(s, g)
 
 
 def inverse_factor(entry):

time: 62.5 us -> 62.4 us (level)
  no operation moved by 1% of the time
where the time goes in v6:
time: 62.4 us; the launch traced here: 62.3 us
  Pallas kernels  61.5 us (99%)
  between operations  0.8 us (1%)
    pallas_call x1, Pallas kernels, local(): pl.pallas_call(functools.partial(sweep_kernel, sizes), out_shape=(pltpu.V...  57.3 us
    pallas_call x1, Pallas kernels, local(): pl.pallas_call(functools.partial(basis_kernel, cells), out_shape=(jax.Sha...  4.18 us

profile of v6, /device:TPU:1, one launch (start us, length us, event | category | flops | bytes accessed | tf_op | source)
XLA Modules:
  0.0 62.3 jit_solution(14727425399519819788)
XLA Ops:
  0.6 57.3 %sweeps.1 = (f32[8,16,16,1024]{3,2,1,0:T(8,128)S(1)}, f32[8,8,8,512]{3,2,1,0:T(8,128)S(1)}, f32[8,128]{1,0:T(8,128)S(1)}) custom-call(s32[2,3]{1,0:T(2,128)} %bitcast.1, f32[8,16,16,1024]{3,2,1,0:T(8,128)} %in_ref.1), custom_call_target="tpu_custom_call" | custom-call | tf_op jit(solution)/shard_map/sweeps/pallas_call | solution.py:527
  58.0 4.2 %basis.1 = (f32[8,16,16,1024]{3,2,1,0:T(8,128)}, f32[8,8,8,512]{3,2,1,0:T(8,128)}) custom-call(f32[8,128]{1,0:T(8,128)S(1)} %get-tuple-element.5.gram_ref, f32[8,16,16,1024]{3,2,1,0:T(8,128)S(1)} %get-tuple-element.6.fields_ref, f32[8,8,8,512]{3,2,1,0:T(8,128)S(1)} %get-tuple-element.7.coarse_ref), custom_call_target="tpu_custom_call" | custom-call | tf_op jit(solution)/shard_map/basis/pallas_call | solution.py:562
